TPU v7x, 256 devices: a whole 4x4x8 slice. The times are simulated.
256 devices in a mesh: panel: 32 (over y, x, core), samp: 8 (over z).
Axes of the slice: x: 4, y: 4, z: 8, core: 2. Of those that a mesh axis runs over, the one named last changes fastest.
Arguments:
- called_allele_tallies: int32 [4096, 1024], P('samp'), may hold values from 0 to 2
- presence_flags: int32 [4096, 1024], P('samp'), may hold values 0 or 1
- reference_panel_strands: int32 [65536, 1024], P('panel'), may hold values from 0 to 1
- softmax_sharpness: float32 [4096], P('samp'), may hold values from 0.02 to 4
- trait_measurements: float32 [4096], P('samp'), may hold values from -8 to 8
- cohort_membership: int32 [4096], P('samp'), may hold values from 0 to 7, as said below
Outputs:
- dosage_out: bfloat16 [4096, 1024], P('samp', 'panel')
- zscore: float32 [1024], P('panel')
Inputs may be any that keep to these rules, and one draw needn't show every extreme that they name: `cohort_membership`: every group id from 0 to 7 occurs.
All inputs are finite; a program needn't handle non-finite values. No bound on the sum of `presence_flags` on one device may be relied on, other than what follows from the above.
Results may differ from a plain program's by a relative error of at most 0.0055.
Values sent between devices are 32-bit elements; how exact they have to be, the bound alone decides.
No kernel may reach another device: no remote copies, remote signals or barrier semaphores. Data moves between devices by JAX's collectives and lax.ppermute only.
A program may use at most 64 MiB of HBM per device.

v0:
```python
import jax
import jax.numpy as jnp
from jax import lax
from jax.sharding import Mesh
from jax.sharding import PartitionSpec as P

GROUPS = 8
PANEL = ("panel_0", "panel_1", "panel_2")


log_two = 0.6931471805599453


def copy_for_each(shard, axis):
    count = lax.axis_size(axis)
    return lax.all_to_all(
        jnp.broadcast_to(shard[None], (count, *shard.shape)), axis, 0, 0, tiled=True
    )


def of_everyone(shard, axis):
    return copy_for_each(shard, axis).sum(axis=0)


def over_copies(shard, axis):
    return copy_for_each(shard, axis).max(axis=0)


def over_axes(shard, axes):
    for axis in axes:
        shard = lax.psum(shard, axis)
    return shard


def in_blocks(shard, dim, count):
    before, after = (shard.shape[:dim], shard.shape[dim + 1 :])
    return jnp.moveaxis(shard.reshape(*before, count, -1, *after), dim, 0)


def sent_and_summed(shard, axis, dim):
    count = lax.axis_size(axis)
    pieces = lax.all_to_all(in_blocks(shard, dim, count), axis, 0, 0, tiled=True)
    return jnp.sum(pieces, axis=0)


def together(arrays, axis):
    line, at, gathered = (jnp.concatenate([a.reshape(-1) for a in arrays]), 0, [])
    so_far = of_everyone(line, axis)
    for a in arrays:
        gathered.append(so_far[at : at + a.size].reshape(a.shape))
        at += a.size
    return tuple(gathered)


def on_device(
    called_allele_tallies,
    presence_flags,
    reference_panel_strands,
    softmax_sharpness,
    trait_measurements,
    cohort_membership,
):
    panel_count = lax.axis_size(PANEL)
    sample_rows, variants = called_allele_tallies.shape
    local_haps = reference_panel_strands.shape[0]
    hap_float = reference_panel_strands.astype(jnp.float32)
    allele_counts = of_everyone(jnp.sum(hap_float, axis=0), PANEL)
    allele_freq = allele_counts / float(local_haps * panel_count)
    geno_float = called_allele_tallies.astype(jnp.float32)
    observed_f = presence_flags.astype(jnp.float32)
    demeaned_expected_count = (observed_f * (geno_float - 2.0 * allele_freq[None, :])).astype(
        jnp.bfloat16
    )
    tile_first_entry = jnp.sum(
        demeaned_expected_count.astype(jnp.float32) * allele_freq[None, :], axis=1
    )
    hap_bf = reference_panel_strands.astype(jnp.bfloat16)
    raw_efficient_statistic = lax.dot_general(
        demeaned_expected_count,
        hap_bf,
        (((1,), (1,)), ((), ())),
        preferred_element_type=jnp.float32,
    )
    panel_match_energies = softmax_sharpness[:, None] * (
        raw_efficient_statistic - tile_first_entry[:, None]
    )
    local_steps = jnp.ceil(jnp.max(panel_match_energies, axis=1) / log_two)
    share = variants // panel_count
    first_column = lax.axis_index(PANEL) * share
    peak_steps = over_copies(local_steps, PANEL)
    weights = jnp.exp(panel_match_energies - log_two * peak_steps[:, None])
    weight_total = over_axes(jnp.sum(weights, axis=1), PANEL)
    partial_dose = 2.0 * jnp.dot(
        weights.astype(jnp.bfloat16), hap_bf, preferred_element_type=jnp.float32
    )
    own_dose = sent_and_summed(partial_dose, PANEL, 1)
    expected_allele_count = own_dose / weight_total[:, None]
    own_geno = lax.dynamic_slice_in_dim(geno_float, first_column, share, 1)
    own_observed = lax.dynamic_slice_in_dim(presence_flags, first_column, share, 1)
    dosage = jnp.where(own_observed == 1, own_geno, expected_allele_count)
    dosage_out = dosage.astype(jnp.bfloat16)
    member = (cohort_membership[:, None] == jnp.arange(GROUPS, dtype=jnp.int32)[None, :]).astype(
        jnp.float32
    )
    group_sum_local = jnp.dot(trait_measurements, member, precision=lax.Precision.HIGHEST)
    group_count_local = jnp.sum(member, axis=0)
    dose_sum_local = jnp.sum(dosage, axis=0)
    dose_square_local = jnp.sum(dosage * dosage, axis=0)
    all_samples = float(sample_rows * lax.axis_size("samp"))
    local_cross = jnp.dot(trait_measurements, dosage, precision=lax.Precision.HIGHEST)
    local_group_dose = jnp.dot(member.T, dosage, precision=lax.Precision.HIGHEST)
    cross, group_dose, dose_sum, dose_square, group_sum, group_count, pheno_square = together(
        (
            local_cross,
            local_group_dose,
            dose_sum_local,
            dose_square_local,
            group_sum_local,
            group_count_local,
            jnp.sum(trait_measurements * trait_measurements),
        ),
        "samp",
    )
    group_mean = group_sum / group_count
    score_u = cross - jnp.dot(group_mean, group_dose, precision=lax.Precision.HIGHEST)
    resid_square = pheno_square - jnp.sum(group_sum * group_mean)
    sigma = resid_square / (all_samples - GROUPS)
    dose_mean = dose_sum / all_samples
    spread = dose_square / all_samples - dose_mean * dose_mean
    zscore = score_u / jnp.sqrt(sigma * all_samples * (spread + 1e-05))
    return (dosage_out, zscore)


def solution(mesh):
    finer = Mesh(
        mesh.devices.reshape(4, 4, 2, mesh.shape["samp"]), ("panel_0", "panel_1", "panel_2", "samp")
    )
    placed = (P("samp", None), P("samp", None), P(PANEL, None), P("samp"), P("samp"), P("samp"))
    return jax.shard_map(
        on_device,
        mesh=finer,
        in_specs=placed,
        out_specs=(P("samp", PANEL), P(PANEL)),
        check_vma=False,
    )
```

profile of v0, /device:TPU:2, one launch (start us, length us, event | category | flops | bytes accessed | tf_op | source)
XLA Modules:
  0.0 122.3 jit_solution(13171496174605333055)
XLA Ops:
  0.6 0.0 copy-start
  0.6 4.2 %convert_reduce_fusion = f32[1024]{0:T(1024)S(1)} fusion(s32[2048,1024]{1,0:T(8,128)} %param.8), kind=kLoop, calls=%fused_computation | loop fusion | flops 4193280 | bytes 8392704 | tf_op jit(solution)/shard_map/reduce_sum | solution.py:67
  4.8 0.7 broadcast_in_dim.6
  5.5 7.6 %all-to-all-start = ((f32[32,1,1024]{2,1,0:T(1,128)}), f32[32,1,1024]{2,1,0:T(1,128)S(1)}, u32[]{:S(2)}, u32[]{:S(2)}) async-start(f32[32,1,1024]{2,1,0:T(1,128)} %broadcast_in_dim.6), calls=%async_computation | async-start | bytes 262144 | tf_op jit(solution)/shard_map/all_to_all | solution.py:16
  13.1 0.0 copy-done
  13.2 1.9 %copy.19 = s32[512,1024]{0,1:T(8,128)} copy(s32[512,1024]{1,0:T(8,128)S(1)} %copy-done) | data formatting | bytes 4194304 | tf_op args[1]
  15.0 0.0 copy-start.3
  15.0 1.9 %copy.20 = s32[512,1024]{0,1:T(8,128)S(1)} copy(s32[512,1024]{1,0:T(8,128)} %param.6) | data formatting | bytes 4194304 | tf_op args[0]
  17.0 2.8 %all-to-all-done = f32[32,1,1024]{2,1,0:T(1,128)S(1)} async-done(((f32[32,1,1024]{2,1,0:T(1,128)}), f32[32,1,1024]{2,1,0:T(1,128)S(1)}, u32[]{:S(2)}, u32[]{:S(2)}) %all-to-all-start) | async-done | bytes 131104 | tf_op jit(solution)/shard_map/all_to_all | solution.py:16
  19.7 0.1 reduce_sum.100
  19.8 2.1 %multiply_reduce_fusion = (f32[512]{0:T(512)S(1)}, bf16[512,1024]{0,1:T(8,128)(2,1)S(1)}) fusion(f32[1024]{0:T(1024)S(1)} %get-tuple-element.8, f32[1024]{0:T(1024)S(1)} %get-tuple-element.7, s32[512,1024]{0,1:T(8,128)S(1)} %copy.20, s32[512,1024]{0,1:T(8,128)} %copy.19), kind=kLoop, calls=%fused_computation.9 | loop fusion | flops 4193792 | bytes 5253120 | tf_op jit(solution)/shard_map/reduce_sum | solution.py:74
  22.0 0.0 copy-done.3
  22.0 7.9 %fusion = (f32[512]{0:T(512)S(1)}, f32[512,2048]{1,0:T(8,128)}) fusion(f32[512]{0:T(512)S(1)} %get-tuple-element.5, f32[512]{0:T(512)S(1)} %copy-done.3, bf16[512,1024]{0,1:T(8,128)(2,1)S(1)} %get-tuple-element.6, s32[2048,1024]{1,0:T(8,128)} %param.8), kind=kOutput, calls=%fused_computation.3 | convolution fusion | flops 2152726016 | bytes 13637632 | tf_op jit(solution)/shard_map/dot_general | solution.py:78
  29.9 10.9 %all_to_all.23 = f32[32,1,512]{2,1,0:T(1,128)S(1)} all-to-all(f32[32,1,512]{2,1,0:T(1,128)S(1)} %broadcast_in_dim.7), channel_id=1, replica_groups=mesh['panel_0'=4,'panel_1'=4,'panel_2'=2,'samp'=8] {'panel_0','panel_1',..., dimensions={0} | all-to-all | bytes 131072 | tf_op jit(solution)/shard_map/all_to_all | solution.py:16
  40.8 0.1 reduce_max.19
  40.9 8.5 %fusion.11 = f32[512,1024]{1,0:T(8,128)} fusion(s32[2048,1024]{1,0:T(8,128)} %param.8, f32[512,2048]{1,0:T(8,128)} %get-tuple-element.10, f32[512]{0:T(512)S(1)} %broadcast_multiply_fusion.2, f32[512]{0:T(512)S(1)} %get-tuple-element.5, f32[512]{0:T(512)S(1)} %copy-done.3), kind=kOutput, calls=%fused_computation.15 | convolution fusion | flops 2154299392 | bytes 14686208 | tf_op jit(solution)/shard_map/dot_general | solution.py:93
  49.4 2.9 %copy.24 = f32[512,1024]{0,1:T(8,128)} copy(f32[512,1024]{1,0:T(8,128)} %fusion.11) | data formatting | bytes 4194304 | tf_op jit(solution)/shard_map/mul | solution.py:93
  52.3 0.0 copy-start.2
  52.3 0.0 copy-start.1
  52.3 5.9 %all-to-all-start.2 = ((f32[32,512,32]{1,2,0:T(8,128)}), f32[32,512,32]{1,2,0:T(8,128)}, u32[]{:S(2)}, u32[]{:S(2)}) async-start(f32[32,512,32]{1,2,0:T(8,128)} %bitcast.26), calls=%async_computation.2 | async-start | bytes 4194304 | tf_op jit(solution)/shard_map/all_to_all | solution.py:42
  58.3 1.6 %convert_element_type.27 = f32[512,1024]{0,1:T(8,128)} convert(s32[512,1024]{0,1:T(8,128)S(1)} %copy.20) | non-fusion elementwise | flops 524288 | bytes 4194304 | tf_op jit(solution)/shard_map/convert_element_type | solution.py:69
  59.9 0.0 copy-done.2
  59.9 0.6 multiply_reduce_fusion.2
  60.5 0.0 copy-done.1
  60.5 0.1 convert_reduce_fusion.1
  60.6 0.1 convolution_bitcast_fusion
  60.7 3.2 %fusion.1 = f32[512]{0:T(512)S(1)} fusion(f32[512,2048]{1,0:T(8,128)} %get-tuple-element.10, f32[512]{0:T(512)S(1)} %broadcast_multiply_fusion.2, f32[512]{0:T(512)S(1)} %get-tuple-element.5, f32[512]{0:T(512)S(1)} %copy-done.3), kind=kLoop, calls=%fused_computation.4 | loop fusion | flops 4193792 | bytes 4202496 | tf_op jit(solution)/shard_map/reduce_sum | solution.py:92
  63.9 22.1 %psum.21 = f32[512]{0:T(512)S(1)} all-reduce(f32[512]{0:T(512)S(1)} %fusion.1), channel_id=1, replica_groups=mesh['panel_0'=4,'panel_1'=4,'panel_2'=2,'samp'=8] {'panel_0'}, use_global_device_ids=true, to_apply=%region_7.0 | all-reduce | flops 512 | bytes 4096 | tf_op jit(solution)/shard_map/psum | solution.py:31
  86.0 9.5 %psum.22 = f32[512]{0:T(512)S(1)} all-reduce(f32[512]{0:T(512)S(1)} %psum.21), channel_id=1, replica_groups=mesh['panel_0'=4,'panel_1'=4,'panel_2'=2,'samp'=8] {'panel_1'}, use_global_device_ids=true, to_apply=%region_8.0 | all-reduce | flops 512 | bytes 4096 | tf_op jit(solution)/shard_map/psum | solution.py:31
  95.6 2.5 %psum.23 = f32[512]{0:T(512)S(1)} all-reduce(f32[512]{0:T(512)S(1)} %psum.22), channel_id=1, replica_groups=mesh['panel_0'=4,'panel_1'=4,'panel_2'=2,'samp'=8] {'panel_2'}, use_global_device_ids=true, to_apply=%region_9.0 | all-reduce | flops 512 | bytes 4096 | tf_op jit(solution)/shard_map/psum | solution.py:31
  98.0 0.0 all-to-all-done.2
  98.0 1.7 %reduce_sum.102 = f32[512,32]{0,1:T(8,128)S(1)} reduce(f32[32,512,32]{1,2,0:T(8,128)} %all-to-all-done.2, f32[]{:T(128)} %constant.45.clone.1), dimensions={0}, to_apply=%region_5.0 | reduce | flops 507904 | bytes 2162692 | tf_op jit(solution)/shard_map/reduce_sum | solution.py:43
  99.7 1.0 multiply_reduce_fusion.1
  100.8 0.1 fusion.18
  100.9 0.2 convolution_bitcast_fusion.1
  101.1 0.1 reshape.57
  101.1 0.8 concatenate.3
  101.9 0.6 broadcast_in_dim.8
  102.5 8.5 %all-to-all-start.3 = ((f32[8,1,369]{2,1,0:T(1,128)}), f32[8,1,369]{2,1,0:T(1,128)S(1)}, u32[]{:S(2)}, u32[]{:S(2)}) async-start(f32[8,1,369]{2,1,0:T(1,128)} %broadcast_in_dim.8), calls=%async_computation.3 | async-start | bytes 24576 | tf_op jit(solution)/shard_map/all_to_all | solution.py:16
  111.0 0.6 convert_element_type.34
  111.6 7.1 %all-to-all-done.3 = f32[8,1,369]{2,1,0:T(1,128)S(1)} async-done(((f32[8,1,369]{2,1,0:T(1,128)}), f32[8,1,369]{2,1,0:T(1,128)S(1)}, u32[]{:S(2)}, u32[]{:S(2)}) %all-to-all-start.3) | async-done | bytes 11840 | tf_op jit(solution)/shard_map/all_to_all | solution.py:16
  118.7 0.6 slice.25
  119.3 0.8 multiply_reduce_fusion.3
  120.1 0.1 slice.24
  120.2 0.1 reshape.59
  121.6 0.7 fusion.17
  (5 shorter events, 0.1 us)
Async XLA Ops:
  0.6 12.5 %copy-start = (s32[512,1024]{1,0:T(8,128)S(1)}, s32[512,1024]{1,0:T(8,128)}, u32[]{:S(2)}) copy-start(s32[512,1024]{1,0:T(8,128)} %param.7) | copy-start | bytes 6291460
  5.5 14.2 %all-to-all-start = ((f32[32,1,1024]{2,1,0:T(1,128)}), f32[32,1,1024]{2,1,0:T(1,128)S(1)}, u32[]{:S(2)}, u32[]{:S(2)}) async-start(f32[32,1,1024]{2,1,0:T(1,128)} %broadcast_in_dim.6), calls=%async_computation | async-start | bytes 262144 | tf_op jit(solution)/shard_map/all_to_all | solution.py:16
  15.0 6.9 %copy-start.3 = (f32[512]{0:T(512)S(1)}, f32[512]{0:T(512)}, u32[]{:S(2)}) copy-start(f32[512]{0:T(512)} %param.9) | copy-start | bytes 6148
  52.3 7.5 %copy-start.2 = (f32[512]{0:T(512)S(1)}, f32[512]{0:T(512)}, u32[]{:S(2)}) copy-start(f32[512]{0:T(512)} %param.10) | copy-start | bytes 6148
  52.3 8.1 %copy-start.1 = (s32[512]{0:T(512)S(1)}, s32[512]{0:T(512)}, u32[]{:S(2)}) copy-start(s32[512]{0:T(512)} %param.11) | copy-start | bytes 6148
  52.3 45.7 %all-to-all-start.2 = ((f32[32,512,32]{1,2,0:T(8,128)}), f32[32,512,32]{1,2,0:T(8,128)}, u32[]{:S(2)}, u32[]{:S(2)}) async-start(f32[32,512,32]{1,2,0:T(8,128)} %bitcast.26), calls=%async_computation.2 | async-start | bytes 4194304 | tf_op jit(solution)/shard_map/all_to_all | solution.py:42
  102.5 16.2 %all-to-all-start.3 = ((f32[8,1,369]{2,1,0:T(1,128)}), f32[8,1,369]{2,1,0:T(1,128)S(1)}, u32[]{:S(2)}, u32[]{:S(2)}) async-start(f32[8,1,369]{2,1,0:T(1,128)} %broadcast_in_dim.8), calls=%async_computation.3 | async-start | bytes 24576 | tf_op jit(solution)/shard_map/all_to_all | solution.py:16
where the time goes:
time: 124 us; the launch traced here: 122 us
  blocking collectives  45.1 us (36%)
  starting transfers between devices  22 us (18%)
  matrix products  17.5 us (14%)
  other arithmetic  16.1 us (13%)
  waiting for transfers between devices  9.91 us (8%)
  local copies, waits for them, and re-layouts  9.63 us (8%)
  between operations  2.06 us (2%)
    psum x3, blocking collectives, over_axes(): shard = lax.psum(shard, axis)  34.1 us
    all_to_all x2, starting transfers between devices, copy_for_each(): lax.all_to_all(jnp.broadcast_to(shard[None], (count, *shard.shape)), axis...  16.1 us
    all_to_all x1, blocking collectives, copy_for_each(): lax.all_to_all(jnp.broadcast_to(shard[None], (count, *shard.shape)), axis...  10.9 us
    all_to_all x2, waiting for transfers between devices, copy_for_each(): lax.all_to_all(jnp.broadcast_to(shard[None], (count, *shard.shape)), axis...  9.91 us
    dot_general x1, matrix products, on_device(): jnp.dot(weights.astype(jnp.bfloat16), hap_bf, preferred_element_type=jnp....  8.51 us
    dot_general x1, matrix products, on_device(): lax.dot_general(demeaned_expected_count, hap_bf, (((1,), (1,)), ((), ()))...  7.89 us
    all_to_all x1, starting transfers between devices, sent_and_summed(): lax.all_to_all(in_blocks(shard, dim, count), axis, 0, 0, tiled=True)  5.9 us
    reduce_sum x1, other arithmetic, on_device(): allele_counts = of_everyone(jnp.sum(hap_float, axis=0), PANEL)  4.17 us
  transfers between devices with their start and end apart: 3, of which 2 were waited for; matrix products, arithmetic and copies ran while one was open for 8% of the time, Pallas kernels for 0%

commit v1 on v0

v1 whole, which is shorter than its diff:
```python
import functools

import jax
import jax.numpy as jnp
from jax import lax
from jax.experimental import pallas as pl
from jax.experimental.pallas import tpu as pltpu
from jax.sharding import Mesh
from jax.sharding import PartitionSpec as P

GROUPS = 8
CHIP_AXES = ("panel_0", "panel_1")
PANEL = ("panel_0", "panel_1", "panel_2")
LOG_TWO = 0.6931471805599453
LOG2_E = 1.4426950408889634
LANES = 128
STATS = 16
MIB = 1 << 20

VMEM = pltpu.VMEM


def in_vmem(x):
    return pltpu.with_memory_space_constraint(x, VMEM)


def whole():
    return pl.BlockSpec(memory_space=VMEM)


def count_kernel(panel, as_bf16, counts, landed, tile, sems):
    rows, variants = panel.shape
    pieces = sems.shape[0]
    step = rows // pieces

    def copy(i):
        span = pl.ds(i * step, step)
        return pltpu.make_async_copy(panel.at[span], landed.at[span], sems.at[i])

    for i in range(pieces):
        copy(i).start()

    total = jnp.zeros((8, variants), jnp.int32)
    for i in range(pieces):
        copy(i).wait()

        def body(r, acc):
            span = pl.ds(pl.multiple_of(i * step + r * 32, 32), 32)
            x = landed[span, :]
            as_bf16[span, :] = x.astype(jnp.float32).astype(jnp.bfloat16)
            return acc + jnp.sum(x.reshape(4, 8, variants), axis=0)

        total = lax.fori_loop(0, step // 32, body, total)
    row = jnp.sum(total.astype(jnp.float32), axis=0, keepdims=True)
    for r in range(variants // LANES):
        tile[r : r + 1, :] = row[:, r * LANES : (r + 1) * LANES]
    one = tile[...]
    for j in range(counts.shape[0]):
        counts[j] = one


def turn_kernel(as_bf16, called, present, turned, own, called_part, present_part, flipped, sems):
    haps, variants = as_bf16.shape
    core = lax.axis_index("panel_2")
    here = (lax.axis_index("panel_0") * lax.axis_size("panel_1") + lax.axis_index("panel_1")) * 2
    here = here + core
    share = own.shape[0]
    per_tile = LANES // share
    lanes = pl.ds(pl.multiple_of((here // per_tile) * LANES, LANES), LANES)
    first = pltpu.make_async_copy(called.at[:, lanes], called_part, sems.at[0])
    second = pltpu.make_async_copy(present.at[:, lanes], present_part, sems.at[1])
    first.start()
    second.start()
    half = variants // 2
    block = 256

    def body(h, carry):
        at = pl.ds(pl.multiple_of(h * block, block), block)
        for t in range(variants // LANES):
            x = as_bf16[at, t * LANES : (t + 1) * LANES].T
            for q in range(per_tile):
                chip = t * (per_tile // 2) + q // 2
                slot = jnp.bitwise_xor(core, q % 2)
                to = pl.ds(pl.multiple_of(slot * half + chip * share, share), share)
                turned[to, at] = x[q * share : (q + 1) * share, :]
        return carry

    lax.fori_loop(0, haps // block, body, 0)
    first.wait()
    second.wait()
    code = jnp.where(present_part[...] == 1, called_part[...].astype(jnp.float32), -1.0)
    flipped[...] = code.T
    own[...] = flipped[pl.ds(pl.multiple_of((here % per_tile) * share, share), share), :]


def impute_kernel(
    haplotypes,
    as_bf16,
    turned,
    counts,
    called,
    present,
    sharpness,
    mine,
    other,
    centred,
    offsets,
    raw,
    weights,
):
    samples, variants = called.shape
    haps = as_bf16.shape[0]
    tiles = samples // LANES
    total = jnp.sum(counts[...], axis=0)
    freq = jnp.concatenate([total[r : r + 1, :] for r in range(variants // LANES)], axis=1)
    freq = freq / haplotypes
    twice = 2.0 * freq

    step = 32

    def centre(r, carry):
        span = pl.ds(pl.multiple_of(r * step, step), step)
        c = present[span, :].astype(jnp.float32) * (called[span, :].astype(jnp.float32) - twice)
        c = c.astype(jnp.bfloat16)
        centred[span, :] = c
        off = jnp.sum(c.astype(jnp.float32) * freq, axis=1, keepdims=True)
        offsets[span, :] = jnp.broadcast_to(off, (step, LANES))
        return carry

    lax.fori_loop(0, samples // step, centre, 0)
    offset = jnp.concatenate(
        [offsets[t * LANES : (t + 1) * LANES, :].T[0:1, :] for t in range(tiles)], axis=1
    )

    raw[...] = lax.dot_general(
        as_bf16[...], centred[...], (((1,), (1,)), ((), ())), preferred_element_type=jnp.float32
    )

    chunk = 64

    def highest(r, best):
        x = raw[pl.ds(pl.multiple_of(r * chunk, chunk), chunk), :]
        return jnp.maximum(best, jnp.max(x.reshape(chunk // 8, 8, samples), axis=0))

    best = lax.fori_loop(
        0, haps // chunk, highest, jnp.full((8, samples), -jnp.inf, jnp.float32)
    )
    best = jnp.max(best, axis=0, keepdims=True)
    heat = sharpness[...]
    peak = heat * (best - offset)
    steps = jnp.ceil(peak / LOG_TWO)
    slope = heat * LOG2_E
    shift = peak * LOG2_E - steps

    def weigh(r, acc):
        span = pl.ds(pl.multiple_of(r * chunk, chunk), chunk)
        w = jnp.exp2(slope * (raw[span, :] - best) + shift)
        weights[span, :] = w.astype(jnp.bfloat16)
        return acc + jnp.sum(w.reshape(chunk // 8, 8, samples), axis=0)

    acc = lax.fori_loop(0, haps // chunk, weigh, jnp.zeros((8, samples), jnp.float32))
    weight_total = jnp.sum(acc, axis=0, keepdims=True)

    blocks = mine.shape[0]
    share = (mine.shape[1] - 2 * tiles) // tiles
    for out, start in ((mine, 0), (other, variants // 2)):
        dose = jnp.dot(
            turned[start : start + variants // 2, :],
            weights[...],
            preferred_element_type=jnp.float32,
        )
        for t in range(tiles):
            lanes = slice(t * LANES, (t + 1) * LANES)
            for k in range(blocks):
                out[k, t * share : (t + 1) * share, :] = dose[k * share : (k + 1) * share, lanes]
        for t in range(tiles):
            lanes = slice(t * LANES, (t + 1) * LANES)
            out[0, tiles * share + t : tiles * share + t + 1, :] = steps[:, lanes]
            out[0, tiles * (share + 1) + t : tiles * (share + 1) + t + 1, :] = weight_total[:, lanes]


def pair_kernel(mine, theirs, both):
    blocks, height, _ = mine.shape
    tiles = 4
    share = height // tiles - 2
    top = tiles * share
    a, b = mine[0, top : top + tiles, :], theirs[0, top : top + tiles, :]
    steps = jnp.maximum(a, b)
    up, down = jnp.exp2(a - steps), jnp.exp2(b - steps)
    total = up * mine[0, top + tiles :, :] + down * theirs[0, top + tiles :, :]
    tail = jnp.concatenate([steps, total], axis=0)
    for k in range(blocks):
        for t in range(tiles):
            span = slice(t * share, (t + 1) * share)
            both[k, span, :] = (
                mine[k, span, :] * up[t : t + 1, :] + theirs[k, span, :] * down[t : t + 1, :]
            )
        both[k, top:, :] = tail


def dose_kernel(parts, own, trait, cohort, dose_out, stats, square):
    blocks, height, _ = parts.shape
    tiles = 4
    share = height // tiles - 2
    top = tiles * share
    sums = [jnp.zeros((share, LANES), jnp.float32) for _ in range(3 + GROUPS)]
    tail = [jnp.zeros((GROUPS, LANES), jnp.float32) for _ in range(3)]
    row = lax.broadcasted_iota(jnp.int32, (GROUPS, LANES), 0)
    steps = jnp.max(parts[:, top : top + tiles, :], axis=0)
    for t in range(tiles):
        lanes = slice(t * LANES, (t + 1) * LANES)
        peak = steps[t : t + 1, :]
        total = jnp.zeros((1, LANES), jnp.float32)
        dose = jnp.zeros((share, LANES), jnp.float32)
        for k in range(blocks):
            scale = jnp.exp2(parts[k, top + t : top + t + 1, :] - peak)
            total += scale * parts[k, top + tiles + t : top + tiles + t + 1, :]
            dose += scale * parts[k, t * share : (t + 1) * share, :]
        called = own[:, lanes]
        dose = jnp.where(called >= 0.0, called, 2.0 * dose / total)
        dose_out[:, lanes] = dose.astype(jnp.bfloat16)
        y, group = trait[:, lanes], cohort[:, lanes]
        sums[0] += y * dose
        sums[1] += dose
        sums[2] += dose * dose
        for g in range(GROUPS):
            sums[3 + g] += jnp.where(group == g, dose, 0.0)
        member = jnp.where(group == row, 1.0, 0.0)
        tail[0] += member * y
        tail[1] += member
        tail[2] += jnp.where(row == 0, y * y, 0.0)
    square[...] = jnp.zeros_like(square)
    lane = lax.broadcasted_iota(jnp.int32, (share, LANES), 1)
    packed = jnp.zeros((share, LANES), jnp.float32)
    for i, s in enumerate(sums):
        packed = jnp.where(lane == i, jnp.sum(s, axis=1, keepdims=True), packed)
    square[0:share, :] = packed
    lane = lax.broadcasted_iota(jnp.int32, (GROUPS, LANES), 1)
    packed = square[0:GROUPS, :]
    for i, s in enumerate(tail):
        packed = jnp.where(lane == 3 + GROUPS + i, jnp.sum(s, axis=1, keepdims=True), packed)
    square[0:GROUPS, :] = packed
    flat = square[...].T[0:STATS, :]
    for j in range(stats.shape[0]):
        stats[j] = flat


def score_kernel(all_samples, stats, zscore):
    s = jnp.sum(stats[...], axis=0)
    cross, dose_sum, dose_square = s[0:1, :], s[1:2, :], s[2:3, :]
    group_dose = s[3 : 3 + GROUPS, :]
    group_sum, group_count = s[3 + GROUPS : 4 + GROUPS, :], s[4 + GROUPS : 5 + GROUPS, :]
    lane = lax.broadcasted_iota(jnp.int32, (1, LANES), 1)
    group_mean = jnp.where(
        lane < GROUPS, group_sum / jnp.where(lane < GROUPS, group_count, 1.0), 0.0
    )
    row = lax.broadcasted_iota(jnp.int32, (GROUPS, LANES), 0)
    col = lax.broadcasted_iota(jnp.int32, (GROUPS, LANES), 1)
    means = jnp.sum(jnp.where(row == col, group_mean, 0.0), axis=1, keepdims=True)
    score_u = cross - jnp.sum(means * group_dose, axis=0, keepdims=True)
    explained = jnp.sum(
        jnp.where(lane < GROUPS, group_sum * group_mean, 0.0), axis=1, keepdims=True
    )
    square = s[5 + GROUPS : 6 + GROUPS, 0:1]
    sigma = (square - explained) / (all_samples - GROUPS)
    mean = dose_sum / all_samples
    spread = dose_square / all_samples - mean * mean
    z = score_u / jnp.sqrt(sigma * all_samples * (spread + 1e-05))
    zscore[...] = z[:, : zscore.shape[1]]


def on_device(called, present, panel, sharpness, trait, cohort):
    f32, bf16 = jnp.float32, jnp.bfloat16
    samples, variants = called.shape
    haps = panel.shape[0]
    devices = lax.axis_size(PANEL)
    chips = lax.axis_size(CHIP_AXES)
    strata = lax.axis_size("samp")
    tiles = samples // LANES
    share = variants // devices
    height = tiles * (share + 2)
    pieces = 16

    as_bf16, counts = pl.pallas_call(
        count_kernel,
        out_shape=(VMEM((haps, variants), bf16), VMEM((devices, 8, LANES), f32)),
        in_specs=[pl.BlockSpec(memory_space=pl.ANY)],
        out_specs=(whole(), whole()),
        scratch_shapes=[
            VMEM((haps, variants), jnp.int32),
            VMEM((8, LANES), f32),
            pltpu.SemaphoreType.DMA((pieces,)),
        ],
        cost_estimate=pl.CostEstimate(flops=10**8, bytes_accessed=haps * variants * 4, transcendentals=0),
        compiler_params=pltpu.CompilerParams(vmem_limit_bytes=12 * MIB),
        name="count",
    )(panel)
    every_count = lax.all_to_all(counts, PANEL, 0, 0, tiled=True)

    turned, own = pl.pallas_call(
        turn_kernel,
        out_shape=(VMEM((variants, haps), bf16), VMEM((share, samples), f32)),
        in_specs=[whole(), pl.BlockSpec(memory_space=pl.ANY), pl.BlockSpec(memory_space=pl.ANY)],
        out_specs=(whole(), whole()),
        scratch_shapes=[
            VMEM((samples, LANES), jnp.int32),
            VMEM((samples, LANES), jnp.int32),
            VMEM((LANES, samples), f32),
            pltpu.SemaphoreType.DMA((2,)),
        ],
        cost_estimate=pl.CostEstimate(flops=10**9, bytes_accessed=haps * variants * 4, transcendentals=0),
        compiler_params=pltpu.CompilerParams(vmem_limit_bytes=4 * MIB),
        name="turn",
    )(as_bf16, called, present)

    mine, other = pl.pallas_call(
        functools.partial(impute_kernel, float(haps * devices)),
        out_shape=(VMEM((chips, height, LANES), f32), VMEM((chips, height, LANES), f32)),
        in_specs=[whole()] * 6,
        out_specs=(whole(), whole()),
        scratch_shapes=[
            VMEM((samples, variants), bf16),
            VMEM((samples, LANES), f32),
            VMEM((haps, samples), f32),
            VMEM((haps, samples), bf16),
        ],
        cost_estimate=pl.CostEstimate(
            flops=4 * samples * variants * haps, bytes_accessed=10**7, transcendentals=samples * haps
        ),
        compiler_params=pltpu.CompilerParams(vmem_limit_bytes=20 * MIB),
        name="impute",
    )(
        as_bf16,
        turned,
        every_count,
        in_vmem(called),
        in_vmem(present),
        sharpness.reshape(1, samples),
    )
    theirs = lax.ppermute(other, "panel_2", [(0, 1), (1, 0)])
    both = pl.pallas_call(
        pair_kernel,
        out_shape=VMEM((chips, height, LANES), f32),
        in_specs=[whole()] * 2,
        out_specs=whole(),
        cost_estimate=pl.CostEstimate(flops=10**7, bytes_accessed=10**6, transcendentals=0),
        compiler_params=pltpu.CompilerParams(vmem_limit_bytes=4 * MIB),
        name="pair",
    )(mine, theirs)
    parts = lax.all_to_all(both, CHIP_AXES, 0, 0, tiled=True)

    dose, stats = pl.pallas_call(
        dose_kernel,
        out_shape=(jax.ShapeDtypeStruct((share, samples), bf16), VMEM((strata, STATS, LANES), f32)),
        in_specs=[whole()] * 4,
        out_specs=(whole(), whole()),
        scratch_shapes=[VMEM((LANES, LANES), f32)],
        cost_estimate=pl.CostEstimate(flops=10**7, bytes_accessed=10**6, transcendentals=0),
        compiler_params=pltpu.CompilerParams(vmem_limit_bytes=6 * MIB),
        name="dose",
    )(parts, own, trait.reshape(1, samples), cohort.reshape(1, samples))
    every_stat = lax.all_to_all(stats, "samp", 0, 0, tiled=True)

    zscore = pl.pallas_call(
        functools.partial(score_kernel, float(samples * strata)),
        out_shape=jax.ShapeDtypeStruct((1, share), f32),
        in_specs=[whole()],
        out_specs=whole(),
        compiler_params=pltpu.CompilerParams(vmem_limit_bytes=4 * MIB),
        name="score",
    )(every_stat)
    return dose.T, zscore.reshape(share)


def solution(mesh):
    finer = Mesh(
        mesh.devices.reshape(4, 4, 2, mesh.shape["samp"]), ("panel_0", "panel_1", "panel_2", "samp")
    )
    placed = (P("samp", None), P("samp", None), P(PANEL, None), P("samp"), P("samp"), P("samp"))
    return jax.shard_map(
        on_device,
        mesh=finer,
        in_specs=placed,
        out_specs=(P("samp", PANEL), P(PANEL)),
        check_vma=False,
    )
```

time: 124 us -> 83.1 us (0.67); the launches traced: 122 us -> 82.7 us
  matrix products: 17.5 us -> 0 us
  other arithmetic: 16.1 us -> 0 us
  starting transfers between devices: 22 us -> 7.82 us
  Pallas kernels: 0 us -> 14 us
  local copies, waits for them, and re-layouts: 9.63 us -> 17.1 us
  waiting for transfers between devices: 9.91 us -> 2.64 us
  blocking collectives: 45.1 us -> 40.5 us
  between operations: 2.06 us -> 0.71 us
    psum x3 -> x0, blocking collectives: 34.1 us -> none  [over_axes(): shard = lax.psum(shard, axis)]
    all_to_all x1 -> x2, blocking collectives: 10.9 us -> 40.5 us  [the longest x1 23.9 us: on_device(): parts = lax.all_to_all(both, CHIP_AXES, 0, 0, tiled=True)]
    dot_general x6 -> x0, matrix products: 17.5 us -> none  [the longest x1 8.51 us: on_device(): jnp.dot(weights.astype(jnp.bfloat16), hap_bf, preferred_element_type=jnp....]
    all_to_all x3 -> x1, starting transfers between devices: 22 us -> 7.62 us  [on_device(): every_count = lax.all_to_all(counts, PANEL, 0, 0, tiled=True)]
    pallas_call x0 -> x6, Pallas kernels: none -> 14 us  [the longest x1 8.12 us: on_device(): pl.pallas_call(functools.partial(impute_kernel, float(haps * devices)), o...]
    reduce_sum x10 -> x0, other arithmetic: 13.8 us -> none  [the longest x1 4.17 us: on_device(): allele_counts = of_everyone(jnp.sum(hap_float, axis=0), PANEL)]
    unnamed x10 -> x24, local copies, waits for them, and re-layouts: 3.81 us -> 17.1 us
    all_to_all x3 -> x1, waiting for transfers between devices: 9.91 us -> 0.01 us  [on_device(): every_count = lax.all_to_all(counts, PANEL, 0, 0, tiled=True)]
  transfers between devices with their start and end apart: 3 -> 2, of which waited for: 2 -> 1; matrix products, arithmetic and copies ran while one was open for 8% -> 0% of each run, Pallas kernels for 0% -> 2%
where the time goes in v1:
time: 83.1 us; the launch traced here: 82.7 us
  blocking collectives  40.5 us (49%)
  local copies, waits for them, and re-layouts  17.1 us (21%)
  Pallas kernels  14 us (17%)
  starting transfers between devices  7.82 us (9%)
  waiting for transfers between devices  2.64 us (3%)
    all_to_all x1, blocking collectives, on_device(): parts = lax.all_to_all(both, CHIP_AXES, 0, 0, tiled=True)  23.9 us
    unnamed x24, local copies, waits for them, and re-layouts  17.1 us
    all_to_all x1, blocking collectives, on_device(): every_stat = lax.all_to_all(stats, 'samp', 0, 0, tiled=True)  16.6 us
    pallas_call x1, Pallas kernels, on_device(): pl.pallas_call(functools.partial(impute_kernel, float(haps * devices)), o...  8.12 us
    all_to_all x1, starting transfers between devices, on_device(): every_count = lax.all_to_all(counts, PANEL, 0, 0, tiled=True)  7.62 us
    ppermute x1, waiting for transfers between devices, on_device(): theirs = lax.ppermute(other, 'panel_2', [(0, 1), (1, 0)])  2.64 us
    pallas_call x1, Pallas kernels, on_device(): pl.pallas_call(count_kernel, out_shape=(VMEM((haps, variants), bf16), VME...  2.45 us
    pallas_call x1, Pallas kernels, on_device(): pl.pallas_call(turn_kernel, out_shape=(VMEM((variants, haps), bf16), VMEM...  1.77 us
  transfers between devices with their start and end apart: 2, of which 1 were waited for; matrix products, arithmetic and copies ran while one was open for 0% of the time, Pallas kernels for 2%

profile of v1, /device:TPU:2, one launch (start us, length us, event | category | flops | bytes accessed | tf_op | source)
XLA Modules:
  0.0 82.7 jit_solution(3966174090122333920)
XLA Ops:
  0.6 0.0 copy-start
  0.6 3.4 %copy-done = s32[2048,1024]{1,0:T(8,128)S(1)} copy-done((s32[2048,1024]{1,0:T(8,128)S(1)}, s32[2048,1024]{1,0:T(8,128)}, u32[]{:S(2)}) %copy-start) | copy-done | bytes 8388632
  4.0 0.0 copy-start.4
  4.0 2.4 %count.1 = (bf16[2048,1024]{1,0:T(8,128)(2,1)S(1)}, f32[32,8,128]{2,1,0:T(8,128)}) custom-call(s32[2048,1024]{1,0:T(8,128)S(1)} %copy-done), custom_call_target="tpu_custom_call" | custom-call | flops 100000000 | bytes 8388608 | tf_op jit(solution)/shard_map/count/pallas_call | solution.py:284
  6.5 0.0 copy-start.1
  6.5 1.9 %copy-done.1 = bf16[2048,1024]{1,0:T(8,128)(2,1)} copy-done((bf16[2048,1024]{1,0:T(8,128)(2,1)}, bf16[2048,1024]{1,0:T(8,128)(2,1)S(1)}, u32[]{:S(2)}) %copy-start.1) | copy-done | bytes 4194328
  8.4 7.6 %all-to-all-start = ((f32[32,8,128]{2,1,0:T(8,128)}), f32[32,8,128]{2,1,0:T(8,128)S(1)}, u32[]{:S(2)}, u32[]{:S(2)}) async-start(f32[32,8,128]{2,1,0:T(8,128)} %get-tuple-element.12), calls=%async_computation | async-start | bytes 262144 | tf_op jit(solution)/shard_map/all_to_all | solution.py:298
  16.1 0.0 copy-done.4
  16.1 0.0 copy-start.2
  16.1 2.2 %copy-done.2 = bf16[2048,1024]{1,0:T(8,128)(2,1)S(1)} copy-done((bf16[2048,1024]{1,0:T(8,128)(2,1)S(1)}, bf16[2048,1024]{1,0:T(8,128)(2,1)}, u32[]{:S(2)}) %copy-start.2) | copy-done | bytes 4194328
  18.3 0.0 copy-start.5
  18.3 1.6 %copy-done.5 = s32[512,1024]{1,0:T(8,128)S(1)} copy-done((s32[512,1024]{1,0:T(8,128)S(1)}, s32[512,1024]{1,0:T(8,128)}, u32[]{:S(2)}) %copy-start.5) | copy-done | bytes 2097176
  19.8 0.0 copy-start.11
  19.8 1.8 %turn.1 = (bf16[1024,2048]{1,0:T(8,128)(2,1)S(1)}, f32[32,512]{1,0:T(8,128)S(1)}) custom-call(bf16[2048,1024]{1,0:T(8,128)(2,1)S(1)} %copy-done.2, s32[512,1024]{1,0:T(8,128)S(1)} %copy-done.4, s32[512,1024]{1,0:T(8,128)S(1)} %copy-done.5), custom_call_target="tpu_custom_call" | custom-call | flops 1000000000 | bytes 8388608 | tf_op jit(solution)/shard_map/turn/pallas_call | solution.py:300
  21.6 0.0 copy-start.9
  21.6 2.0 %copy-done.9 = bf16[1024,2048]{1,0:T(8,128)(2,1)} copy-done((bf16[1024,2048]{1,0:T(8,128)(2,1)}, bf16[1024,2048]{1,0:T(8,128)(2,1)S(1)}, u32[]{:S(2)}) %copy-start.9) | copy-done | bytes 4194328
  23.6 0.0 all-to-all-done.counts
  23.6 0.0 copy-done.11
  23.6 0.0 copy-start.3
  23.6 2.2 %copy-done.3 = bf16[2048,1024]{1,0:T(8,128)(2,1)S(1)} copy-done((bf16[2048,1024]{1,0:T(8,128)(2,1)S(1)}, bf16[2048,1024]{1,0:T(8,128)(2,1)}, u32[]{:S(2)}) %copy-start.3) | copy-done | bytes 4194328
  25.8 0.0 copy-start.6
  25.8 1.6 %copy-done.6 = s32[512,1024]{1,0:T(8,128)S(1)} copy-done((s32[512,1024]{1,0:T(8,128)S(1)}, s32[512,1024]{1,0:T(8,128)}, u32[]{:S(2)}) %copy-start.6) | copy-done | bytes 2097176
  27.4 0.0 copy-start.10
  27.4 2.2 %copy-done.10 = bf16[1024,2048]{1,0:T(8,128)(2,1)S(1)} copy-done((bf16[1024,2048]{1,0:T(8,128)(2,1)S(1)}, bf16[1024,2048]{1,0:T(8,128)(2,1)}, u32[]{:S(2)}) %copy-start.10) | copy-done | bytes 4194328
  29.6 8.1 %impute.1 = (f32[16,136,128]{2,1,0:T(8,128)S(1)}, f32[16,136,128]{2,1,0:T(8,128)S(1)}) custom-call(bf16[2048,1024]{1,0:T(8,128)(2,1)S(1)} %copy-done.3, bf16[1024,2048]{1,0:T(8,128)(2,1)S(1)} %copy-done.10, f32[32,8,128]{2,1,0:T(8,128)S(1)} %all-to-all-done.counts, s32[512,1024]{1,0:T(8,128)S(1)} %copy-done.4, s32[512,1024]{1,0:T(8,128)S(1)} %copy-done.6, ...), custom_call_target="tpu_custom_call" | custom-call | flops 4294967296 | bytes 10000000 | tf_op jit(solution)/shard_map/impute/pallas_call | solution.py:316
  37.7 0.2 collective-permute-start
  37.9 2.6 %collective-permute-done.theirs = f32[16,136,128]{2,1,0:T(8,128)S(1)} collective-permute-done((f32[16,136,128]{2,1,0:T(8,128)S(1)}, f32[16,136,128]{2,1,0:T(8,128)S(1)}, u32[]{:S(2)}, u32[]{:S(2)}) %collective-permute-start) | collective-permute-done | bytes 1114144 | tf_op jit(solution)/shard_map/ppermute | solution.py:340
  40.6 0.0 copy-start.7
  40.6 0.0 copy-start.8
  40.6 0.1 pair.1
  40.7 23.9 %all_to_all.15.parts = f32[16,136,128]{2,1,0:T(8,128)S(1)} all-to-all(f32[16,136,128]{2,1,0:T(8,128)S(1)} %pair.1), channel_id=1, replica_groups=mesh['panel_0'=4,'panel_1'=4,'panel_2'=2,'samp'=8] {'panel_0','panel_1'}, dimensions={0} | all-to-all | bytes 2228224 | tf_op jit(solution)/shard_map/all_to_all | solution.py:350
  64.6 0.0 copy-done.7
  64.6 0.0 copy-done.8
  64.6 0.8 dose.1
  65.4 16.6 %all_to_all.16.stats = f32[8,16,128]{2,1,0:T(8,128)S(1)} all-to-all(f32[8,16,128]{2,1,0:T(8,128)S(1)} %get-tuple-element.17), channel_id=1, replica_groups=mesh['panel_0'=4,'panel_1'=4,'panel_2'=2,'samp'=8] {'samp'}, dimensions={0} | all-to-all | bytes 131072 | tf_op jit(solution)/shard_map/all_to_all | solution.py:362
  82.0 0.7 score.1
Async XLA Ops:
  0.6 3.4 %copy-start = (s32[2048,1024]{1,0:T(8,128)S(1)}, s32[2048,1024]{1,0:T(8,128)}, u32[]{:S(2)}) copy-start(s32[2048,1024]{1,0:T(8,128)} %panel.1) | copy-start | bytes 25165828
  4.0 12.0 %copy-start.4 = (s32[512,1024]{1,0:T(8,128)S(1)}, s32[512,1024]{1,0:T(8,128)}, u32[]{:S(2)}) copy-start(s32[512,1024]{1,0:T(8,128)} %called.3) | copy-start | bytes 6291460
  6.5 2.0 %copy-start.1 = (bf16[2048,1024]{1,0:T(8,128)(2,1)}, bf16[2048,1024]{1,0:T(8,128)(2,1)S(1)}, u32[]{:S(2)}) copy-start(bf16[2048,1024]{1,0:T(8,128)(2,1)S(1)} %get-tuple-element.10.as_bf16) | copy-start | bytes 12582916
  8.4 15.2 %all-to-all-start = ((f32[32,8,128]{2,1,0:T(8,128)}), f32[32,8,128]{2,1,0:T(8,128)S(1)}, u32[]{:S(2)}, u32[]{:S(2)}) async-start(f32[32,8,128]{2,1,0:T(8,128)} %get-tuple-element.12), calls=%async_computation | async-start | bytes 262144 | tf_op jit(solution)/shard_map/all_to_all | solution.py:298
  16.1 2.2 %copy-start.2 = (bf16[2048,1024]{1,0:T(8,128)(2,1)S(1)}, bf16[2048,1024]{1,0:T(8,128)(2,1)}, u32[]{:S(2)}) copy-start(bf16[2048,1024]{1,0:T(8,128)(2,1)} %copy-done.1) | copy-start | bytes 12582916
  18.3 1.6 %copy-start.5 = (s32[512,1024]{1,0:T(8,128)S(1)}, s32[512,1024]{1,0:T(8,128)}, u32[]{:S(2)}) copy-start(s32[512,1024]{1,0:T(8,128)} %present.3) | copy-start | bytes 6291460
  19.8 3.8 %copy-start.11 = (f32[512]{0:T(512)S(1)}, f32[512]{0:T(512)}, u32[]{:S(2)}) copy-start(f32[512]{0:T(512)} %param.9) | copy-start | bytes 6148
  21.6 2.0 %copy-start.9 = (bf16[1024,2048]{1,0:T(8,128)(2,1)}, bf16[1024,2048]{1,0:T(8,128)(2,1)S(1)}, u32[]{:S(2)}) copy-start(bf16[1024,2048]{1,0:T(8,128)(2,1)S(1)} %get-tuple-element.11.turned) | copy-start | bytes 12582916
  23.6 2.2 %copy-start.3 = (bf16[2048,1024]{1,0:T(8,128)(2,1)S(1)}, bf16[2048,1024]{1,0:T(8,128)(2,1)}, u32[]{:S(2)}) copy-start(bf16[2048,1024]{1,0:T(8,128)(2,1)} %copy-done.1) | copy-start | bytes 12582916
  25.8 1.6 %copy-start.6 = (s32[512,1024]{1,0:T(8,128)S(1)}, s32[512,1024]{1,0:T(8,128)}, u32[]{:S(2)}) copy-start(s32[512,1024]{1,0:T(8,128)} %present.3) | copy-start | bytes 6291460
  27.4 2.2 %copy-start.10 = (bf16[1024,2048]{1,0:T(8,128)(2,1)S(1)}, bf16[1024,2048]{1,0:T(8,128)(2,1)}, u32[]{:S(2)}) copy-start(bf16[1024,2048]{1,0:T(8,128)(2,1)} %copy-done.9) | copy-start | bytes 12582916
  37.7 2.8 %collective-permute-start = (f32[16,136,128]{2,1,0:T(8,128)S(1)}, f32[16,136,128]{2,1,0:T(8,128)S(1)}, u32[]{:S(2)}, u32[]{:S(2)}) collective-permute-start(f32[16,136,128]{2,1,0:T(8,128)S(1)} %get-tuple-element.14), channel_id=1, source_target_pairs={{0,8},{8,0},{1,9},{9,1},{2,10},{10,2},{3,11},{11,3},{4,12},{12,4},... | collective-permute-start | bytes 3342344 | tf_op jit(solution)/shard_map/ppermute | solution.py:340
  40.6 24.0 %copy-start.7 = (f32[512]{0:T(512)S(1)}, f32[512]{0:T(512)}, u32[]{:S(2)}) copy-start(f32[512]{0:T(512)} %param.10) | copy-start | bytes 6148
  40.6 24.0 %copy-start.8 = (s32[512]{0:T(512)S(1)}, s32[512]{0:T(512)}, u32[]{:S(2)}) copy-start(s32[512]{0:T(512)} %param.11) | copy-start | bytes 6148

commit v2 on v1

--- a/solution.py
+++ b/solution.py
@@ -24,73 +24,101 @@
     return pltpu.with_memory_space_constraint(x, VMEM)
 
 
+def in_hbm(x):
+    return pltpu.with_memory_space_constraint(x, pltpu.HBM)
+
+
 def whole():
     return pl.BlockSpec(memory_space=VMEM)
 
 
-def count_kernel(panel, as_bf16, counts, landed, tile, sems):
+def count_kernel(
+    panel,
+    called,
+    present,
+    as_bf16,
+    turned,
+    counts,
+    own,
+    landed,
+    tile,
+    called_part,
+    present_part,
+    flipped,
+    sems,
+    own_sems,
+):
     rows, variants = panel.shape
     pieces = sems.shape[0]
     step = rows // pieces
 
     def copy(i):
-        span = pl.ds(i * step, step)
+        span = pl.ds(pl.multiple_of(i * step, step), step)
         return pltpu.make_async_copy(panel.at[span], landed.at[span], sems.at[i])
 
     for i in range(pieces):
         copy(i).start()
 
-    total = jnp.zeros((8, variants), jnp.int32)
-    for i in range(pieces):
-        copy(i).wait()
-
-        def body(r, acc):
-            span = pl.ds(pl.multiple_of(i * step + r * 32, 32), 32)
-            x = landed[span, :]
-            as_bf16[span, :] = x.astype(jnp.float32).astype(jnp.bfloat16)
-            return acc + jnp.sum(x.reshape(4, 8, variants), axis=0)
-
-        total = lax.fori_loop(0, step // 32, body, total)
-    row = jnp.sum(total.astype(jnp.float32), axis=0, keepdims=True)
-    for r in range(variants // LANES):
-        tile[r : r + 1, :] = row[:, r * LANES : (r + 1) * LANES]
-    one = tile[...]
-    for j in range(counts.shape[0]):
-        counts[j] = one
-
-
-def turn_kernel(as_bf16, called, present, turned, own, called_part, present_part, flipped, sems):
-    haps, variants = as_bf16.shape
     core = lax.axis_index("panel_2")
     here = (lax.axis_index("panel_0") * lax.axis_size("panel_1") + lax.axis_index("panel_1")) * 2
     here = here + core
     share = own.shape[0]
     per_tile = LANES // share
     lanes = pl.ds(pl.multiple_of((here // per_tile) * LANES, LANES), LANES)
-    first = pltpu.make_async_copy(called.at[:, lanes], called_part, sems.at[0])
-    second = pltpu.make_async_copy(present.at[:, lanes], present_part, sems.at[1])
+    first = pltpu.make_async_copy(called.at[:, lanes], called_part, own_sems.at[0])
+    second = pltpu.make_async_copy(present.at[:, lanes], present_part, own_sems.at[1])
     first.start()
     second.start()
     half = variants // 2
-    block = 256
-
-    def body(h, carry):
-        at = pl.ds(pl.multiple_of(h * block, block), block)
+
+    def piece(i, acc):
+        copy(i).wait()
+        at = pl.ds(pl.multiple_of(i * step, step), step)
         for t in range(variants // LANES):
-            x = as_bf16[at, t * LANES : (t + 1) * LANES].T
+            cols = slice(t * LANES, (t + 1) * LANES)
+            x = landed[at, cols]
+            acc[t] = acc[t] + jnp.sum(x.reshape(step // 8, 8, LANES), axis=0)
+            x = x.astype(jnp.float32).astype(jnp.bfloat16)
+            as_bf16[at, cols] = x
+            x = x.T
             for q in range(per_tile):
                 chip = t * (per_tile // 2) + q // 2
                 slot = jnp.bitwise_xor(core, q % 2)
                 to = pl.ds(pl.multiple_of(slot * half + chip * share, share), share)
                 turned[to, at] = x[q * share : (q + 1) * share, :]
-        return carry
-
-    lax.fori_loop(0, haps // block, body, 0)
+        return acc
+
+    zero = [jnp.zeros((8, LANES), jnp.int32) for _ in range(variants // LANES)]
+    total = lax.fori_loop(0, pieces, piece, zero)
+    for r in range(variants // LANES):
+        tile[r : r + 1, :] = jnp.sum(total[r].astype(jnp.float32), axis=0, keepdims=True)
+    one = tile[...]
+    for j in range(counts.shape[0]):
+        counts[j] = one
     first.wait()
     second.wait()
     code = jnp.where(present_part[...] == 1, called_part[...].astype(jnp.float32), -1.0)
     flipped[...] = code.T
     own[...] = flipped[pl.ds(pl.multiple_of((here % per_tile) * share, share), share), :]
+
+
+def freq_row(counts, haplotypes, variants):
+    total = jnp.sum(counts[...], axis=0)
+    rows = [total[r : r + 1, :] for r in range(variants // LANES)]
+    return jnp.concatenate(rows, axis=1) / haplotypes
+
+
+def store_half(out, dose, steps, weight_total):
+    tiles = dose.shape[1] // LANES
+    blocks, height, _ = out.shape
+    share = height // tiles - 2
+    for t in range(tiles):
+        lanes = slice(t * LANES, (t + 1) * LANES)
+        for k in range(blocks):
+            out[k, t * share : (t + 1) * share, :] = dose[k * share : (k + 1) * share, lanes]
+        top = tiles * share + t
+        out[0, top : top + 1, :] = steps[:, lanes]
+        out[0, top + tiles : top + tiles + 1, :] = weight_total[:, lanes]
 
 
 def impute_kernel(
@@ -101,42 +129,48 @@
     called,
     present,
     sharpness,
-    mine,
     other,
+    weights,
+    scales,
     centred,
     offsets,
     raw,
-    weights,
 ):
     samples, variants = called.shape
     haps = as_bf16.shape[0]
     tiles = samples // LANES
-    total = jnp.sum(counts[...], axis=0)
-    freq = jnp.concatenate([total[r : r + 1, :] for r in range(variants // LANES)], axis=1)
-    freq = freq / haplotypes
+    freq = freq_row(counts, haplotypes, variants)
     twice = 2.0 * freq
 
-    step = 32
+    step = 64
 
     def centre(r, carry):
         span = pl.ds(pl.multiple_of(r * step, step), step)
-        c = present[span, :].astype(jnp.float32) * (called[span, :].astype(jnp.float32) - twice)
-        c = c.astype(jnp.bfloat16)
-        centred[span, :] = c
-        off = jnp.sum(c.astype(jnp.float32) * freq, axis=1, keepdims=True)
-        offsets[span, :] = jnp.broadcast_to(off, (step, LANES))
+        part = jnp.zeros((step, LANES), jnp.float32)
+        for t in range(variants // LANES):
+            cols = slice(t * LANES, (t + 1) * LANES)
+            c = called[span, cols].astype(jnp.float32) - twice[:, cols]
+            c = present[span, cols].astype(jnp.float32) * c
+            c = c.astype(jnp.bfloat16)
+            centred[span, cols] = c
+            part += c.astype(jnp.float32) * freq[:, cols]
+        offsets[span, :] = part
         return carry
 
     lax.fori_loop(0, samples // step, centre, 0)
     offset = jnp.concatenate(
-        [offsets[t * LANES : (t + 1) * LANES, :].T[0:1, :] for t in range(tiles)], axis=1
+        [
+            jnp.sum(offsets[t * LANES : (t + 1) * LANES, :].T, axis=0, keepdims=True)
+            for t in range(tiles)
+        ],
+        axis=1,
     )
 
     raw[...] = lax.dot_general(
         as_bf16[...], centred[...], (((1,), (1,)), ((), ())), preferred_element_type=jnp.float32
     )
 
-    chunk = 64
+    chunk = 128
 
     def highest(r, best):
         x = raw[pl.ds(pl.multiple_of(r * chunk, chunk), chunk), :]
@@ -160,23 +194,18 @@
 
     acc = lax.fori_loop(0, haps // chunk, weigh, jnp.zeros((8, samples), jnp.float32))
     weight_total = jnp.sum(acc, axis=0, keepdims=True)
-
-    blocks = mine.shape[0]
-    share = (mine.shape[1] - 2 * tiles) // tiles
-    for out, start in ((mine, 0), (other, variants // 2)):
-        dose = jnp.dot(
-            turned[start : start + variants // 2, :],
-            weights[...],
-            preferred_element_type=jnp.float32,
-        )
-        for t in range(tiles):
-            lanes = slice(t * LANES, (t + 1) * LANES)
-            for k in range(blocks):
-                out[k, t * share : (t + 1) * share, :] = dose[k * share : (k + 1) * share, lanes]
-        for t in range(tiles):
-            lanes = slice(t * LANES, (t + 1) * LANES)
-            out[0, tiles * share + t : tiles * share + t + 1, :] = steps[:, lanes]
-            out[0, tiles * (share + 1) + t : tiles * (share + 1) + t + 1, :] = weight_total[:, lanes]
+    scales[0:1, :] = steps
+    scales[1:2, :] = weight_total
+    dose = jnp.dot(
+        turned[variants // 2 :, :], weights[...], preferred_element_type=jnp.float32
+    )
+    store_half(other, dose, steps, weight_total)
+
+
+def mine_kernel(turned, weights, scales, mine):
+    half = turned.shape[0] // 2
+    dose = jnp.dot(turned[:half, :], weights[...], preferred_element_type=jnp.float32)
+    store_half(mine, dose, scales[0:1, :], scales[1:2, :])
 
 
 def pair_kernel(mine, theirs, both):
@@ -281,53 +310,47 @@
     height = tiles * (share + 2)
     pieces = 16
 
-    as_bf16, counts = pl.pallas_call(
+    hbm = pl.BlockSpec(memory_space=pltpu.HBM)
+    as_bf16, turned, counts, own = pl.pallas_call(
         count_kernel,
-        out_shape=(VMEM((haps, variants), bf16), VMEM((devices, 8, LANES), f32)),
-        in_specs=[pl.BlockSpec(memory_space=pl.ANY)],
-        out_specs=(whole(), whole()),
+        out_shape=(
+            VMEM((haps, variants), bf16),
+            VMEM((variants, haps), bf16),
+            VMEM((devices, 8, LANES), f32),
+            VMEM((share, samples), f32),
+        ),
+        in_specs=[hbm] * 3,
+        out_specs=(whole(),) * 4,
         scratch_shapes=[
             VMEM((haps, variants), jnp.int32),
             VMEM((8, LANES), f32),
-            pltpu.SemaphoreType.DMA((pieces,)),
-        ],
-        cost_estimate=pl.CostEstimate(flops=10**8, bytes_accessed=haps * variants * 4, transcendentals=0),
-        compiler_params=pltpu.CompilerParams(vmem_limit_bytes=12 * MIB),
-        name="count",
-    )(panel)
-    every_count = lax.all_to_all(counts, PANEL, 0, 0, tiled=True)
-
-    turned, own = pl.pallas_call(
-        turn_kernel,
-        out_shape=(VMEM((variants, haps), bf16), VMEM((share, samples), f32)),
-        in_specs=[whole(), pl.BlockSpec(memory_space=pl.ANY), pl.BlockSpec(memory_space=pl.ANY)],
-        out_specs=(whole(), whole()),
-        scratch_shapes=[
             VMEM((samples, LANES), jnp.int32),
             VMEM((samples, LANES), jnp.int32),
             VMEM((LANES, samples), f32),
+            pltpu.SemaphoreType.DMA((pieces,)),
             pltpu.SemaphoreType.DMA((2,)),
         ],
         cost_estimate=pl.CostEstimate(flops=10**9, bytes_accessed=haps * variants * 4, transcendentals=0),
-        compiler_params=pltpu.CompilerParams(vmem_limit_bytes=4 * MIB),
-        name="turn",
-    )(as_bf16, called, present)
-
-    mine, other = pl.pallas_call(
+        compiler_params=pltpu.CompilerParams(vmem_limit_bytes=14 * MIB),
+        name="count",
+    )(in_hbm(panel), in_hbm(called), in_hbm(present))
+    every_count = lax.all_to_all(counts, PANEL, 0, 0, tiled=True)
+
+    block = VMEM((chips, height, LANES), f32)
+    other, weights, scales = pl.pallas_call(
         functools.partial(impute_kernel, float(haps * devices)),
-        out_shape=(VMEM((chips, height, LANES), f32), VMEM((chips, height, LANES), f32)),
+        out_shape=(block, VMEM((haps, samples), bf16), VMEM((8, samples), f32)),
         in_specs=[whole()] * 6,
-        out_specs=(whole(), whole()),
+        out_specs=(whole(),) * 3,
         scratch_shapes=[
             VMEM((samples, variants), bf16),
             VMEM((samples, LANES), f32),
             VMEM((haps, samples), f32),
-            VMEM((haps, samples), bf16),
         ],
         cost_estimate=pl.CostEstimate(
-            flops=4 * samples * variants * haps, bytes_accessed=10**7, transcendentals=samples * haps
+            flops=3 * samples * variants * haps, bytes_accessed=10**7, transcendentals=samples * haps
         ),
-        compiler_params=pltpu.CompilerParams(vmem_limit_bytes=20 * MIB),
+        compiler_params=pltpu.CompilerParams(vmem_limit_bytes=16 * MIB),
         name="impute",
     )(
         as_bf16,
@@ -338,6 +361,17 @@
         sharpness.reshape(1, samples),
     )
     theirs = lax.ppermute(other, "panel_2", [(0, 1), (1, 0)])
+    mine = pl.pallas_call(
+        mine_kernel,
+        out_shape=block,
+        in_specs=[whole()] * 3,
+        out_specs=whole(),
+        cost_estimate=pl.CostEstimate(
+            flops=samples * variants * haps, bytes_accessed=10**6, transcendentals=0
+        ),
+        compiler_params=pltpu.CompilerParams(vmem_limit_bytes=4 * MIB),
+        name="mine",
+    )(turned, weights, scales)
     both = pl.pallas_call(
         pair_kernel,
         out_shape=VMEM((chips, height, LANES), f32),
@@ -351,7 +385,7 @@
 
     dose, stats = pl.pallas_call(
         dose_kernel,
-        out_shape=(jax.ShapeDtypeStruct((share, samples), bf16), VMEM((strata, STATS, LANES), f32)),
+        out_shape=(VMEM((share, samples), bf16), VMEM((strata, STATS, LANES), f32)),
         in_specs=[whole()] * 4,
         out_specs=(whole(), whole()),
         scratch_shapes=[VMEM((LANES, LANES), f32)],

time: 83.1 us -> 67.3 us (0.81)
  local copies, waits for them, and re-layouts: 17.1 us -> 0.64 us
  waiting for transfers between devices: 2.64 us -> 9.09 us
  blocking collectives: 40.5 us -> 35.3 us
  Pallas kernels: 14 us -> 12.6 us
  starting transfers between devices: 7.82 us -> 8.71 us
    unnamed x24 -> x11, local copies, waits for them, and re-layouts: 17.1 us -> 0.64 us
    all_to_all x1, waiting for transfers between devices: 0.01 us -> 7.76 us  [on_device(): every_stat = lax.all_to_all(stats, 'samp', 0, 0, tiled=True)]
    all_to_all x1, blocking collectives: 16.6 us -> 14 us  [on_device(): every_count = lax.all_to_all(counts, PANEL, 0, 0, tiled=True)]
    all_to_all x1, blocking collectives: 23.9 us -> 21.3 us  [on_device(): parts = lax.all_to_all(both, CHIP_AXES, 0, 0, tiled=True)]
    pallas_call x1, Pallas kernels: 8.12 us -> 5.59 us  [on_device(): pl.pallas_call(functools.partial(impute_kernel, float(haps * devices)), o...]
    pallas_call x1, Pallas kernels: 2.45 us -> 3.98 us  [on_device(): pl.pallas_call(count_kernel, out_shape=(VMEM((haps, variants), bf16), VME...]
    ppermute x1, waiting for transfers between devices: 2.64 us -> 1.33 us  [on_device(): theirs = lax.ppermute(other, 'panel_2', [(0, 1), (1, 0)])]
    all_to_all x1, starting transfers between devices: 7.62 us -> 8.47 us  [on_device(): every_stat = lax.all_to_all(stats, 'samp', 0, 0, tiled=True)]
  transfers between devices with their start and end apart: 2 -> 2, of which waited for: 1 -> 2; matrix products, arithmetic and copies ran while one was open for 0% -> 1% of each run, Pallas kernels for 2% -> 2%
where the time goes in v2:
time: 67.3 us; the launch traced here: 67.1 us
  blocking collectives  35.3 us (52%)
  Pallas kernels  12.6 us (19%)
  waiting for transfers between devices  9.09 us (14%)
  starting transfers between devices  8.71 us (13%)
  between operations  0.7 us (1%)
    all_to_all x1, blocking collectives, on_device(): parts = lax.all_to_all(both, CHIP_AXES, 0, 0, tiled=True)  21.3 us
    all_to_all x1, blocking collectives, on_device(): every_count = lax.all_to_all(counts, PANEL, 0, 0, tiled=True)  14 us
    all_to_all x1, starting transfers between devices, on_device(): every_stat = lax.all_to_all(stats, 'samp', 0, 0, tiled=True)  8.47 us
    all_to_all x1, waiting for transfers between devices, on_device(): every_stat = lax.all_to_all(stats, 'samp', 0, 0, tiled=True)  7.76 us
    pallas_call x1, Pallas kernels, on_device(): pl.pallas_call(functools.partial(impute_kernel, float(haps * devices)), o...  5.59 us
    pallas_call x1, Pallas kernels, on_device(): pl.pallas_call(count_kernel, out_shape=(VMEM((haps, variants), bf16), VME...  3.98 us
  transfers between devices with their start and end apart: 2, of which 2 were waited for; matrix products, arithmetic and copies ran while one was open for 1% of the time, Pallas kernels for 2%

profile of v2, /device:TPU:2, one launch (start us, length us, event | category | flops | bytes accessed | tf_op | source)
XLA Modules:
  0.0 67.1 jit_solution(18275525785075429029)
XLA Ops:
  0.6 0.0 copy-start.1
  0.6 0.0 copy-start
  0.7 0.0 copy-start.4
  0.7 4.0 %count.1 = (bf16[2048,1024]{1,0:T(8,128)(2,1)S(1)}, bf16[1024,2048]{1,0:T(8,128)(2,1)S(1)}, f32[32,8,128]{2,1,0:T(8,128)S(1)}, f32[32,512]{1,0:T(8,128)S(1)}) custom-call(s32[2048,1024]{1,0:T(8,128)} %panel.1, s32[512,1024]{1,0:T(8,128)} %called.3, s32[512,1024]{1,0:T(8,128)} %present.3), custom_call_target="tpu_custom_call" | custom-call | flops 1000000000 | bytes 8388608 | tf_op jit(solution)/shard_map/count/pallas_call | solution.py:314
  4.7 14.0 %all_to_all.15.counts = f32[32,8,128]{2,1,0:T(8,128)S(1)} all-to-all(f32[32,8,128]{2,1,0:T(8,128)S(1)} %get-tuple-element.13), channel_id=1, replica_groups=mesh['panel_0'=4,'panel_1'=4,'panel_2'=2,'samp'=8] {'panel_0','panel_1',..., dimensions={0} | all-to-all | bytes 262144 | tf_op jit(solution)/shard_map/all_to_all | solution.py:337
  18.7 0.0 copy-done.1
  18.7 0.0 copy-done
  18.7 0.0 copy-done.4
  18.7 5.6 %impute.1 = (f32[16,136,128]{2,1,0:T(8,128)S(1)}, bf16[2048,512]{1,0:T(8,128)(2,1)S(1)}, f32[8,512]{1,0:T(8,128)S(1)}) custom-call(bf16[2048,1024]{1,0:T(8,128)(2,1)S(1)} %get-tuple-element.12.as_bf16, bf16[1024,2048]{1,0:T(8,128)(2,1)S(1)} %get-tuple-element.11.turned, f32[32,8,128]{2,1,0:T(8,128)S(1)} %all_to_all.15.counts, s32[512,1024]{1,0:T(8,128)S(1)} %copy-done, ...), custom_call_target="tpu_custom_call" | custom-call | flops 3221225472 | bytes 10000000 | tf_op jit(solution)/shard_map/impute/pallas_call | solution.py:340
  24.3 0.2 collective-permute-start
  24.5 1.2 %mine.1 = f32[16,136,128]{2,1,0:T(8,128)S(1)} custom-call(bf16[1024,2048]{1,0:T(8,128)(2,1)S(1)} %get-tuple-element.11.turned, bf16[2048,512]{1,0:T(8,128)(2,1)S(1)} %get-tuple-element.14.weights, f32[8,512]{1,0:T(8,128)S(1)} %get-tuple-element.15.scales), custom_call_target="tpu_custom_call" | custom-call | flops 1073741824 | bytes 1000000 | tf_op jit(solution)/shard_map/mine/pallas_call | solution.py:364
  25.8 0.0 copy-start.2
  25.8 0.0 copy-start.3
  25.8 1.3 %collective-permute-done.theirs = f32[16,136,128]{2,1,0:T(8,128)S(1)} collective-permute-done((f32[16,136,128]{2,1,0:T(8,128)S(1)}, f32[16,136,128]{2,1,0:T(8,128)S(1)}, u32[]{:S(2)}, u32[]{:S(2)}) %collective-permute-start) | collective-permute-done | bytes 1114144 | tf_op jit(solution)/shard_map/ppermute | solution.py:363
  27.1 0.1 pair.1
  27.2 21.3 %all_to_all.16.parts = f32[16,136,128]{2,1,0:T(8,128)S(1)} all-to-all(f32[16,136,128]{2,1,0:T(8,128)S(1)} %pair.1), channel_id=1, replica_groups=mesh['panel_0'=4,'panel_1'=4,'panel_2'=2,'samp'=8] {'panel_0','panel_1'}, dimensions={0} | all-to-all | bytes 2228224 | tf_op jit(solution)/shard_map/all_to_all | solution.py:384
  48.6 0.0 copy-done.2
  48.6 0.0 copy-done.3
  48.6 1.0 %dose.1 = (bf16[32,512]{1,0:T(8,128)(2,1)S(1)}, f32[8,16,128]{2,1,0:T(8,128)}) custom-call(f32[16,136,128]{2,1,0:T(8,128)S(1)} %all_to_all.16.parts, f32[32,512]{1,0:T(8,128)S(1)} %get-tuple-element.17.own, f32[1,512]{1,0:T(1,128)S(1)} %bitcast.6, s32[1,512]{1,0:T(1,128)S(1)} %bitcast.7), custom_call_target="tpu_custom_call" | custom-call | flops 10000000 | bytes 1000000 | tf_op jit(solution)/shard_map/dose/pallas_call | solution.py:386
  49.6 8.5 %all-to-all-start.2 = ((f32[8,16,128]{2,1,0:T(8,128)}), f32[8,16,128]{2,1,0:T(8,128)S(1)}, u32[]{:S(2)}, u32[]{:S(2)}) async-start(f32[8,16,128]{2,1,0:T(8,128)} %get-tuple-element.19), calls=%async_computation.2 | async-start | bytes 131072 | tf_op jit(solution)/shard_map/all_to_all | solution.py:396
  58.0 0.6 copy.8
  58.6 7.8 %all-to-all-done.2.stats = f32[8,16,128]{2,1,0:T(8,128)S(1)} async-done(((f32[8,16,128]{2,1,0:T(8,128)}), f32[8,16,128]{2,1,0:T(8,128)S(1)}, u32[]{:S(2)}, u32[]{:S(2)}) %all-to-all-start.2) | async-done | bytes 65568 | tf_op jit(solution)/shard_map/all_to_all | solution.py:396
  66.4 0.7 %score.1 = f32[1,32]{1,0:T(1,128)} custom-call(f32[8,16,128]{2,1,0:T(8,128)S(1)} %all-to-all-done.2.stats), custom_call_target="tpu_custom_call" | custom-call | tf_op jit(solution)/shard_map/score/pallas_call | solution.py:398
Async XLA Ops:
  0.6 18.0 %copy-start.1 = (s32[512,1024]{1,0:T(8,128)S(1)}, s32[512,1024]{1,0:T(8,128)}, u32[]{:S(2)}) copy-start(s32[512,1024]{1,0:T(8,128)} %present.3) | copy-start | bytes 6291460
  0.6 18.0 %copy-start = (s32[512,1024]{1,0:T(8,128)S(1)}, s32[512,1024]{1,0:T(8,128)}, u32[]{:S(2)}) copy-start(s32[512,1024]{1,0:T(8,128)} %called.3) | copy-start | bytes 6291460
  0.7 18.0 %copy-start.4 = (f32[512]{0:T(512)S(1)}, f32[512]{0:T(512)}, u32[]{:S(2)}) copy-start(f32[512]{0:T(512)} %param.9) | copy-start | bytes 6148
  24.3 2.8 %collective-permute-start = (f32[16,136,128]{2,1,0:T(8,128)S(1)}, f32[16,136,128]{2,1,0:T(8,128)S(1)}, u32[]{:S(2)}, u32[]{:S(2)}) collective-permute-start(f32[16,136,128]{2,1,0:T(8,128)S(1)} %get-tuple-element.16), channel_id=1, source_target_pairs={{0,8},{8,0},{1,9},{9,1},{2,10},{10,2},{3,11},{11,3},{4,12},{12,4},... | collective-permute-start | bytes 3342344 | tf_op jit(solution)/shard_map/ppermute | solution.py:363
  25.8 22.8 %copy-start.2 = (f32[512]{0:T(512)S(1)}, f32[512]{0:T(512)}, u32[]{:S(2)}) copy-start(f32[512]{0:T(512)} %param.10) | copy-start | bytes 6148
  25.8 22.8 %copy-start.3 = (s32[512]{0:T(512)S(1)}, s32[512]{0:T(512)}, u32[]{:S(2)}) copy-start(s32[512]{0:T(512)} %param.11) | copy-start | bytes 6148
  49.6 16.8 %all-to-all-start.2 = ((f32[8,16,128]{2,1,0:T(8,128)}), f32[8,16,128]{2,1,0:T(8,128)S(1)}, u32[]{:S(2)}, u32[]{:S(2)}) async-start(f32[8,16,128]{2,1,0:T(8,128)} %get-tuple-element.19), calls=%async_computation.2 | async-start | bytes 131072 | tf_op jit(solution)/shard_map/all_to_all | solution.py:396

commit v3 on v2

--- a/solution.py
+++ b/solution.py
@@ -14,7 +14,7 @@
 LOG_TWO = 0.6931471805599453
 LOG2_E = 1.4426950408889634
 LANES = 128
-STATS = 16
+STATS = 4
 MIB = 1 << 20
 
 VMEM = pltpu.VMEM
@@ -32,22 +32,7 @@
     return pl.BlockSpec(memory_space=VMEM)
 
 
-def count_kernel(
-    panel,
-    called,
-    present,
-    as_bf16,
-    turned,
-    counts,
-    own,
-    landed,
-    tile,
-    called_part,
-    present_part,
-    flipped,
-    sems,
-    own_sems,
-):
+def count_kernel(panel, as_bf16, turned, counts, landed, tile, sems):
     rows, variants = panel.shape
     pieces = sems.shape[0]
     step = rows // pieces
@@ -60,15 +45,8 @@
         copy(i).start()
 
     core = lax.axis_index("panel_2")
-    here = (lax.axis_index("panel_0") * lax.axis_size("panel_1") + lax.axis_index("panel_1")) * 2
-    here = here + core
-    share = own.shape[0]
+    share = variants // counts.shape[0]
     per_tile = LANES // share
-    lanes = pl.ds(pl.multiple_of((here // per_tile) * LANES, LANES), LANES)
-    first = pltpu.make_async_copy(called.at[:, lanes], called_part, own_sems.at[0])
-    second = pltpu.make_async_copy(present.at[:, lanes], present_part, own_sems.at[1])
-    first.start()
-    second.start()
     half = variants // 2
 
     def piece(i, acc):
@@ -95,11 +73,6 @@
     one = tile[...]
     for j in range(counts.shape[0]):
         counts[j] = one
-    first.wait()
-    second.wait()
-    code = jnp.where(present_part[...] == 1, called_part[...].astype(jnp.float32), -1.0)
-    flipped[...] = code.T
-    own[...] = flipped[pl.ds(pl.multiple_of((here % per_tile) * share, share), share), :]
 
 
 def freq_row(counts, haplotypes, variants):
@@ -108,15 +81,20 @@
     return jnp.concatenate(rows, axis=1) / haplotypes
 
 
-def store_half(out, dose, steps, weight_total):
+def store_half(out, dose):
     tiles = dose.shape[1] // LANES
-    blocks, height, _ = out.shape
-    share = height // tiles - 2
+    share = out.shape[1] // tiles - 2
+    for t in range(tiles):
+        span = slice(t * share, (t + 1) * share)
+        for k in range(out.shape[0]):
+            out[k, span, :] = dose[k * share : (k + 1) * share, t * LANES : (t + 1) * LANES]
+
+
+def store_tail(out, steps, weight_total):
+    tiles = steps.shape[1] // LANES
     for t in range(tiles):
         lanes = slice(t * LANES, (t + 1) * LANES)
-        for k in range(blocks):
-            out[k, t * share : (t + 1) * share, :] = dose[k * share : (k + 1) * share, lanes]
-        top = tiles * share + t
+        top = out.shape[1] - 2 * tiles + t
         out[0, top : top + 1, :] = steps[:, lanes]
         out[0, top + tiles : top + tiles + 1, :] = weight_total[:, lanes]
 
@@ -166,19 +144,11 @@
         axis=1,
     )
 
-    raw[...] = lax.dot_general(
+    product = lax.dot_general(
         as_bf16[...], centred[...], (((1,), (1,)), ((), ())), preferred_element_type=jnp.float32
     )
-
-    chunk = 128
-
-    def highest(r, best):
-        x = raw[pl.ds(pl.multiple_of(r * chunk, chunk), chunk), :]
-        return jnp.maximum(best, jnp.max(x.reshape(chunk // 8, 8, samples), axis=0))
-
-    best = lax.fori_loop(
-        0, haps // chunk, highest, jnp.full((8, samples), -jnp.inf, jnp.float32)
-    )
+    raw[...] = product
+    best = jnp.max(product.reshape(haps // 8, 8, samples), axis=0)
     best = jnp.max(best, axis=0, keepdims=True)
     heat = sharpness[...]
     peak = heat * (best - offset)
@@ -186,6 +156,8 @@
     slope = heat * LOG2_E
     shift = peak * LOG2_E - steps
 
+    chunk = 128
+
     def weigh(r, acc):
         span = pl.ds(pl.multiple_of(r * chunk, chunk), chunk)
         w = jnp.exp2(slope * (raw[span, :] - best) + shift)
@@ -196,16 +168,32 @@
     weight_total = jnp.sum(acc, axis=0, keepdims=True)
     scales[0:1, :] = steps
     scales[1:2, :] = weight_total
-    dose = jnp.dot(
-        turned[variants // 2 :, :], weights[...], preferred_element_type=jnp.float32
-    )
-    store_half(other, dose, steps, weight_total)
-
-
-def mine_kernel(turned, weights, scales, mine):
+    dose = jnp.dot(turned[variants // 2 :, :], weights[...], preferred_element_type=jnp.float32)
+    store_half(other, dose)
+    store_tail(other, steps, weight_total)
+
+
+def mine_kernel(
+    turned, weights, scales, called, present, mine, own, called_part, present_part, flipped, sems
+):
+    here = (lax.axis_index("panel_0") * lax.axis_size("panel_1") + lax.axis_index("panel_1")) * 2
+    here = here + lax.axis_index("panel_2")
+    share = own.shape[0]
+    per_tile = LANES // share
+    lanes = pl.ds(pl.multiple_of((here // per_tile) * LANES, LANES), LANES)
+    first = pltpu.make_async_copy(called.at[:, lanes], called_part, sems.at[0])
+    second = pltpu.make_async_copy(present.at[:, lanes], present_part, sems.at[1])
+    first.start()
+    second.start()
     half = turned.shape[0] // 2
     dose = jnp.dot(turned[:half, :], weights[...], preferred_element_type=jnp.float32)
-    store_half(mine, dose, scales[0:1, :], scales[1:2, :])
+    store_half(mine, dose)
+    store_tail(mine, scales[0:1, :], scales[1:2, :])
+    first.wait()
+    second.wait()
+    code = jnp.where(present_part[...] == 1, called_part[...].astype(jnp.float32), -1.0)
+    flipped[...] = code.T
+    own[...] = flipped[pl.ds(pl.multiple_of((here % per_tile) * share, share), share), :]
 
 
 def pair_kernel(mine, theirs, both):
@@ -227,7 +215,7 @@
         both[k, top:, :] = tail
 
 
-def dose_kernel(parts, own, trait, cohort, dose_out, stats, square):
+def dose_kernel(parts, own, trait, cohort, rounded, stats, square):
     blocks, height, _ = parts.shape
     tiles = 4
     share = height // tiles - 2
@@ -247,7 +235,7 @@
             dose += scale * parts[k, t * share : (t + 1) * share, :]
         called = own[:, lanes]
         dose = jnp.where(called >= 0.0, called, 2.0 * dose / total)
-        dose_out[:, lanes] = dose.astype(jnp.bfloat16)
+        rounded[:, lanes] = dose.astype(jnp.bfloat16)
         y, group = trait[:, lanes], cohort[:, lanes]
         sums[0] += y * dose
         sums[1] += dose
@@ -258,44 +246,56 @@
         tail[0] += member * y
         tail[1] += member
         tail[2] += jnp.where(row == 0, y * y, 0.0)
-    square[...] = jnp.zeros_like(square)
+    sums = [jnp.sum(x, axis=1, keepdims=True) for x in sums]
     lane = lax.broadcasted_iota(jnp.int32, (share, LANES), 1)
-    packed = jnp.zeros((share, LANES), jnp.float32)
-    for i, s in enumerate(sums):
-        packed = jnp.where(lane == i, jnp.sum(s, axis=1, keepdims=True), packed)
-    square[0:share, :] = packed
+    for q in range(LANES // share):
+        packed = jnp.zeros((share, LANES), jnp.float32)
+        for i in range(q, len(sums), LANES // share):
+            packed = jnp.where(lane == i // (LANES // share), sums[i], packed)
+        square[q * share : (q + 1) * share, :] = packed
     lane = lax.broadcasted_iota(jnp.int32, (GROUPS, LANES), 1)
-    packed = square[0:GROUPS, :]
-    for i, s in enumerate(tail):
-        packed = jnp.where(lane == 3 + GROUPS + i, jnp.sum(s, axis=1, keepdims=True), packed)
-    square[0:GROUPS, :] = packed
+    row, first = divmod(len(sums), LANES // share)
+    for i, x in enumerate(tail):
+        span = slice(first * share + i * GROUPS, first * share + (i + 1) * GROUPS)
+        x = jnp.sum(x, axis=1, keepdims=True)
+        square[span, :] = jnp.where(lane == row, x, square[span, :])
     flat = square[...].T[0:STATS, :]
     for j in range(stats.shape[0]):
         stats[j] = flat
 
 
-def score_kernel(all_samples, stats, zscore):
+def score_kernel(all_samples, stats, rounded, zscore, dose_out, line, sems):
+    doses_leave = pltpu.make_async_copy(rounded, dose_out, sems.at[0])
+    scores_leave = pltpu.make_async_copy(line, zscore, sems.at[1])
+    doses_leave.start()
+    share = zscore.shape[1]
     s = jnp.sum(stats[...], axis=0)
-    cross, dose_sum, dose_square = s[0:1, :], s[1:2, :], s[2:3, :]
-    group_dose = s[3 : 3 + GROUPS, :]
-    group_sum, group_count = s[3 + GROUPS : 4 + GROUPS, :], s[4 + GROUPS : 5 + GROUPS, :]
+    parts = [s] + [pltpu.roll(s, LANES - q * share, axis=1) for q in range(1, LANES // share)]
+
+    def stat(i):
+        row, q = divmod(i, len(parts))
+        return parts[q][row : row + 1, :]
+
+    cross, dose_sum, dose_square = stat(0), stat(1), stat(2)
+    group_dose = jnp.concatenate([stat(3 + g) for g in range(GROUPS)], axis=0)
+    tail = stat(3 + GROUPS)
     lane = lax.broadcasted_iota(jnp.int32, (1, LANES), 1)
-    group_mean = jnp.where(
-        lane < GROUPS, group_sum / jnp.where(lane < GROUPS, group_count, 1.0), 0.0
-    )
     row = lax.broadcasted_iota(jnp.int32, (GROUPS, LANES), 0)
     col = lax.broadcasted_iota(jnp.int32, (GROUPS, LANES), 1)
-    means = jnp.sum(jnp.where(row == col, group_mean, 0.0), axis=1, keepdims=True)
-    score_u = cross - jnp.sum(means * group_dose, axis=0, keepdims=True)
-    explained = jnp.sum(
-        jnp.where(lane < GROUPS, group_sum * group_mean, 0.0), axis=1, keepdims=True
-    )
-    square = s[5 + GROUPS : 6 + GROUPS, 0:1]
+    group_sum = jnp.sum(jnp.where(col == row, tail, 0.0), axis=1, keepdims=True)
+    group_count = jnp.sum(jnp.where(col == row + GROUPS, tail, 0.0), axis=1, keepdims=True)
+    square = jnp.sum(jnp.where(lane == 2 * GROUPS, tail, 0.0), axis=1, keepdims=True)
+    group_mean = group_sum / group_count
+    score_u = cross - jnp.sum(group_mean * group_dose, axis=0, keepdims=True)
+    explained = jnp.sum(group_sum * group_mean, axis=0, keepdims=True)
     sigma = (square - explained) / (all_samples - GROUPS)
     mean = dose_sum / all_samples
     spread = dose_square / all_samples - mean * mean
     z = score_u / jnp.sqrt(sigma * all_samples * (spread + 1e-05))
-    zscore[...] = z[:, : zscore.shape[1]]
+    line[...] = z[:, :share]
+    scores_leave.start()
+    doses_leave.wait()
+    scores_leave.wait()
 
 
 def on_device(called, present, panel, sharpness, trait, cohort):
@@ -311,29 +311,24 @@
     pieces = 16
 
     hbm = pl.BlockSpec(memory_space=pltpu.HBM)
-    as_bf16, turned, counts, own = pl.pallas_call(
+    as_bf16, turned, counts = pl.pallas_call(
         count_kernel,
         out_shape=(
             VMEM((haps, variants), bf16),
             VMEM((variants, haps), bf16),
             VMEM((devices, 8, LANES), f32),
-            VMEM((share, samples), f32),
         ),
-        in_specs=[hbm] * 3,
-        out_specs=(whole(),) * 4,
+        in_specs=[hbm],
+        out_specs=(whole(),) * 3,
         scratch_shapes=[
             VMEM((haps, variants), jnp.int32),
             VMEM((8, LANES), f32),
-            VMEM((samples, LANES), jnp.int32),
-            VMEM((samples, LANES), jnp.int32),
-            VMEM((LANES, samples), f32),
             pltpu.SemaphoreType.DMA((pieces,)),
-            pltpu.SemaphoreType.DMA((2,)),
         ],
         cost_estimate=pl.CostEstimate(flops=10**9, bytes_accessed=haps * variants * 4, transcendentals=0),
         compiler_params=pltpu.CompilerParams(vmem_limit_bytes=14 * MIB),
         name="count",
-    )(in_hbm(panel), in_hbm(called), in_hbm(present))
+    )(in_hbm(panel))
     every_count = lax.all_to_all(counts, PANEL, 0, 0, tiled=True)
 
     block = VMEM((chips, height, LANES), f32)
@@ -361,17 +356,23 @@
         sharpness.reshape(1, samples),
     )
     theirs = lax.ppermute(other, "panel_2", [(0, 1), (1, 0)])
-    mine = pl.pallas_call(
+    mine, own = pl.pallas_call(
         mine_kernel,
-        out_shape=block,
-        in_specs=[whole()] * 3,
-        out_specs=whole(),
+        out_shape=(block, VMEM((share, samples), f32)),
+        in_specs=[whole()] * 3 + [hbm] * 2,
+        out_specs=(whole(),) * 2,
+        scratch_shapes=[
+            VMEM((samples, LANES), jnp.int32),
+            VMEM((samples, LANES), jnp.int32),
+            VMEM((LANES, samples), f32),
+            pltpu.SemaphoreType.DMA((2,)),
+        ],
         cost_estimate=pl.CostEstimate(
             flops=samples * variants * haps, bytes_accessed=10**6, transcendentals=0
         ),
-        compiler_params=pltpu.CompilerParams(vmem_limit_bytes=4 * MIB),
+        compiler_params=pltpu.CompilerParams(vmem_limit_bytes=6 * MIB),
         name="mine",
-    )(turned, weights, scales)
+    )(turned, weights, scales, in_hbm(called), in_hbm(present))
     both = pl.pallas_call(
         pair_kernel,
         out_shape=VMEM((chips, height, LANES), f32),
@@ -383,7 +384,7 @@
     )(mine, theirs)
     parts = lax.all_to_all(both, CHIP_AXES, 0, 0, tiled=True)
 
-    dose, stats = pl.pallas_call(
+    rounded, stats = pl.pallas_call(
         dose_kernel,
         out_shape=(VMEM((share, samples), bf16), VMEM((strata, STATS, LANES), f32)),
         in_specs=[whole()] * 4,
@@ -395,14 +396,15 @@
     )(parts, own, trait.reshape(1, samples), cohort.reshape(1, samples))
     every_stat = lax.all_to_all(stats, "samp", 0, 0, tiled=True)
 
-    zscore = pl.pallas_call(
+    zscore, dose = pl.pallas_call(
         functools.partial(score_kernel, float(samples * strata)),
-        out_shape=jax.ShapeDtypeStruct((1, share), f32),
-        in_specs=[whole()],
-        out_specs=whole(),
+        out_shape=(pltpu.HBM((1, share), f32), pltpu.HBM((share, samples), bf16)),
+        in_specs=[whole()] * 2,
+        out_specs=(hbm, hbm),
+        scratch_shapes=[VMEM((1, share), f32), pltpu.SemaphoreType.DMA((2,))],
         compiler_params=pltpu.CompilerParams(vmem_limit_bytes=4 * MIB),
         name="score",
-    )(every_stat)
+    )(every_stat, rounded)
     return dose.T, zscore.reshape(share)
 
 

time: 67.3 us -> 65.4 us (0.972)
  blocking collectives: 35.3 us -> 51.4 us
  waiting for transfers between devices: 9.09 us -> 0.49 us
  starting transfers between devices: 8.71 us -> 0.24 us
    all_to_all x0 -> x1, blocking collectives: none -> 16 us  [on_device(): every_stat = lax.all_to_all(stats, 'samp', 0, 0, tiled=True)]
    all_to_all x1 -> x0, starting transfers between devices: 8.47 us -> none  [on_device(): every_stat = lax.all_to_all(stats, 'samp', 0, 0, tiled=True)]
    all_to_all x1 -> x0, waiting for transfers between devices: 7.76 us -> none  [on_device(): every_stat = lax.all_to_all(stats, 'samp', 0, 0, tiled=True)]
    pallas_call x1, Pallas kernels: 1.24 us -> 2.09 us  [on_device(): pl.pallas_call(mine_kernel, out_shape=(block, VMEM((share, samples), f32)...]
    ppermute x1, waiting for transfers between devices: 1.33 us -> 0.49 us  [on_device(): theirs = lax.ppermute(other, 'panel_2', [(0, 1), (1, 0)])]
  transfers between devices with their start and end apart: 2 -> 1, of which waited for: 2 -> 1; matrix products, arithmetic and copies ran while one was open for 1% -> 0% of each run, Pallas kernels for 2% -> 3%
where the time goes in v3:
time: 65.4 us; the launch traced here: 65.2 us
  blocking collectives  51.4 us (79%)
  Pallas kernels  12.3 us (19%)
  between operations  0.69 us (1%)
    all_to_all x1, blocking collectives, on_device(): parts = lax.all_to_all(both, CHIP_AXES, 0, 0, tiled=True)  21.3 us
    all_to_all x1, blocking collectives, on_device(): every_stat = lax.all_to_all(stats, 'samp', 0, 0, tiled=True)  16 us
    all_to_all x1, blocking collectives, on_device(): every_count = lax.all_to_all(counts, PANEL, 0, 0, tiled=True)  14 us
    pallas_call x1, Pallas kernels, on_device(): pl.pallas_call(functools.partial(impute_kernel, float(haps * devices)), o...  5.25 us
    pallas_call x1, Pallas kernels, on_device(): pl.pallas_call(count_kernel, out_shape=(VMEM((haps, variants), bf16), VME...  3.82 us
    pallas_call x1, Pallas kernels, on_device(): pl.pallas_call(mine_kernel, out_shape=(block, VMEM((share, samples), f32)...  2.09 us
  transfers between devices with their start and end apart: 1, of which 1 were waited for; matrix products, arithmetic and copies ran while one was open for 0% of the time, Pallas kernels for 3%

profile of v3, /device:TPU:2, one launch (start us, length us, event | category | flops | bytes accessed | tf_op | source)
XLA Modules:
  0.0 65.2 jit_solution(7983924570554134649)
XLA Ops:
  0.6 0.0 copy-start.1
  0.6 0.0 copy-start
  0.7 0.0 copy-start.4
  0.7 3.8 %count.1 = (bf16[2048,1024]{1,0:T(8,128)(2,1)S(1)}, bf16[1024,2048]{1,0:T(8,128)(2,1)S(1)}, f32[32,8,128]{2,1,0:T(8,128)S(1)}) custom-call(s32[2048,1024]{1,0:T(8,128)} %panel.1), custom_call_target="tpu_custom_call" | custom-call | flops 1000000000 | bytes 8388608 | tf_op jit(solution)/shard_map/count/pallas_call | solution.py:314
  4.5 14.0 %all_to_all.15.counts = f32[32,8,128]{2,1,0:T(8,128)S(1)} all-to-all(f32[32,8,128]{2,1,0:T(8,128)S(1)} %get-tuple-element.16), channel_id=1, replica_groups=mesh['panel_0'=4,'panel_1'=4,'panel_2'=2,'samp'=8] {'panel_0','panel_1',..., dimensions={0} | all-to-all | bytes 262144 | tf_op jit(solution)/shard_map/all_to_all | solution.py:332
  18.5 0.0 copy-done.1
  18.5 0.0 copy-done
  18.5 0.0 copy-done.4
  18.5 5.2 %impute.1 = (f32[16,136,128]{2,1,0:T(8,128)S(1)}, bf16[2048,512]{1,0:T(8,128)(2,1)S(1)}, f32[8,512]{1,0:T(8,128)S(1)}) custom-call(bf16[2048,1024]{1,0:T(8,128)(2,1)S(1)} %get-tuple-element.15.as_bf16, bf16[1024,2048]{1,0:T(8,128)(2,1)S(1)} %get-tuple-element.14.turned, f32[32,8,128]{2,1,0:T(8,128)S(1)} %all_to_all.15.counts, s32[512,1024]{1,0:T(8,128)S(1)} %copy-done, ...), custom_call_target="tpu_custom_call" | custom-call | flops 3221225472 | bytes 10000000 | tf_op jit(solution)/shard_map/impute/pallas_call | solution.py:335
  23.8 0.2 collective-permute-start
  24.0 2.1 %mine.1 = (f32[16,136,128]{2,1,0:T(8,128)S(1)}, f32[32,512]{1,0:T(8,128)S(1)}) custom-call(bf16[1024,2048]{1,0:T(8,128)(2,1)S(1)} %get-tuple-element.14.turned, bf16[2048,512]{1,0:T(8,128)(2,1)S(1)} %get-tuple-element.17.weights, f32[8,512]{1,0:T(8,128)S(1)} %get-tuple-element.18.scales, s32[512,1024]{1,0:T(8,128)} %called.3, s32[512,1024]{1,0:T(8,128)} %present.3), custom_call_target="tpu_custom_call" | custom-call | flops 1073741824 | bytes 1000000 | tf_op jit(solution)/shard_map/mine/pallas_call | solution.py:359
  26.1 0.5 collective-permute-done.theirs
  26.6 0.0 copy-start.2
  26.6 0.0 copy-start.3
  26.6 0.1 pair.1
  26.7 21.3 %all_to_all.16.parts = f32[16,136,128]{2,1,0:T(8,128)S(1)} all-to-all(f32[16,136,128]{2,1,0:T(8,128)S(1)} %pair.1), channel_id=1, replica_groups=mesh['panel_0'=4,'panel_1'=4,'panel_2'=2,'samp'=8] {'panel_0','panel_1'}, dimensions={0} | all-to-all | bytes 2228224 | tf_op jit(solution)/shard_map/all_to_all | solution.py:385
  48.1 0.0 copy-done.2
  48.1 0.0 copy-done.3
  48.1 0.3 dose.1
  48.4 16.0 %all_to_all.17.stats = f32[8,4,128]{2,1,0:T(4,128)S(1)} all-to-all(f32[8,4,128]{2,1,0:T(4,128)S(1)} %get-tuple-element.22), channel_id=1, replica_groups=mesh['panel_0'=4,'panel_1'=4,'panel_2'=2,'samp'=8] {'samp'}, dimensions={0} | all-to-all | bytes 32768 | tf_op jit(solution)/shard_map/all_to_all | solution.py:397
  64.4 0.7 %score.1 = (f32[1,32]{1,0:T(1,128)}, bf16[32,512]{1,0:T(8,128)(2,1)}) custom-call(f32[8,4,128]{2,1,0:T(4,128)S(1)} %all_to_all.17.stats, bf16[32,512]{1,0:T(8,128)(2,1)S(1)} %get-tuple-element.23.rounded), custom_call_target="tpu_custom_call" | custom-call | tf_op jit(solution)/shard_map/score/pallas_call | solution.py:399
Async XLA Ops:
  0.6 17.9 %copy-start.1 = (s32[512,1024]{1,0:T(8,128)S(1)}, s32[512,1024]{1,0:T(8,128)}, u32[]{:S(2)}) copy-start(s32[512,1024]{1,0:T(8,128)} %present.3) | copy-start | bytes 6291460
  0.6 17.9 %copy-start = (s32[512,1024]{1,0:T(8,128)S(1)}, s32[512,1024]{1,0:T(8,128)}, u32[]{:S(2)}) copy-start(s32[512,1024]{1,0:T(8,128)} %called.3) | copy-start | bytes 6291460
  0.7 17.9 %copy-start.4 = (f32[512]{0:T(512)S(1)}, f32[512]{0:T(512)}, u32[]{:S(2)}) copy-start(f32[512]{0:T(512)} %param.9) | copy-start | bytes 6148
  23.8 2.8 %collective-permute-start = (f32[16,136,128]{2,1,0:T(8,128)S(1)}, f32[16,136,128]{2,1,0:T(8,128)S(1)}, u32[]{:S(2)}, u32[]{:S(2)}) collective-permute-start(f32[16,136,128]{2,1,0:T(8,128)S(1)} %get-tuple-element.20), channel_id=1, source_target_pairs={{0,8},{8,0},{1,9},{9,1},{2,10},{10,2},{3,11},{11,3},{4,12},{12,4},... | collective-permute-start | bytes 3342344 | tf_op jit(solution)/shard_map/ppermute | solution.py:358
  26.6 21.5 %copy-start.2 = (f32[512]{0:T(512)S(1)}, f32[512]{0:T(512)}, u32[]{:S(2)}) copy-start(f32[512]{0:T(512)} %param.10) | copy-start | bytes 6148
  26.6 21.5 %copy-start.3 = (s32[512]{0:T(512)S(1)}, s32[512]{0:T(512)}, u32[]{:S(2)}) copy-start(s32[512]{0:T(512)} %param.11) | copy-start | bytes 6148

commit v4 on v3

--- a/solution.py
+++ b/solution.py
@@ -15,6 +15,7 @@
 LOG2_E = 1.4426950408889634
 LANES = 128
 STATS = 4
+EXTRA = 16
 MIB = 1 << 20
 
 VMEM = pltpu.VMEM
@@ -111,12 +112,10 @@
     weights,
     scales,
     centred,
-    offsets,
     raw,
 ):
     samples, variants = called.shape
     haps = as_bf16.shape[0]
-    tiles = samples // LANES
     freq = freq_row(counts, haplotypes, variants)
     twice = 2.0 * freq
 
@@ -124,29 +123,28 @@
 
     def centre(r, carry):
         span = pl.ds(pl.multiple_of(r * step, step), step)
-        part = jnp.zeros((step, LANES), jnp.float32)
         for t in range(variants // LANES):
             cols = slice(t * LANES, (t + 1) * LANES)
             c = called[span, cols].astype(jnp.float32) - twice[:, cols]
-            c = present[span, cols].astype(jnp.float32) * c
-            c = c.astype(jnp.bfloat16)
-            centred[span, cols] = c
-            part += c.astype(jnp.float32) * freq[:, cols]
-        offsets[span, :] = part
+            c = jnp.where(present[span, cols] == 1, c, 0.0)
+            centred[span, cols] = c.astype(jnp.bfloat16)
         return carry
 
     lax.fori_loop(0, samples // step, centre, 0)
-    offset = jnp.concatenate(
-        [
-            jnp.sum(offsets[t * LANES : (t + 1) * LANES, :].T, axis=0, keepdims=True)
-            for t in range(tiles)
-        ],
-        axis=1,
+
+    high = freq.astype(jnp.bfloat16).astype(jnp.float32)
+    middle = (freq - high).astype(jnp.bfloat16).astype(jnp.float32)
+    row = lax.broadcasted_iota(jnp.int32, (EXTRA, variants), 0)
+    extra = jnp.where(row == 0, high, jnp.where(row == 1, middle, freq - high - middle))
+    extra = jnp.where(row < 3, extra, 0.0).astype(jnp.bfloat16)
+    product = lax.dot_general(
+        jnp.concatenate([as_bf16[...], extra], axis=0),
+        centred[...],
+        (((1,), (1,)), ((), ())),
+        preferred_element_type=jnp.float32,
     )
-
-    product = lax.dot_general(
-        as_bf16[...], centred[...], (((1,), (1,)), ((), ())), preferred_element_type=jnp.float32
-    )
+    offset = jnp.sum(product[haps:, :], axis=0, keepdims=True)
+    product = product[:haps, :]
     raw[...] = product
     best = jnp.max(product.reshape(haps // 8, 8, samples), axis=0)
     best = jnp.max(best, axis=0, keepdims=True)
@@ -154,13 +152,13 @@
     peak = heat * (best - offset)
     steps = jnp.ceil(peak / LOG_TWO)
     slope = heat * LOG2_E
-    shift = peak * LOG2_E - steps
+    shift = peak * LOG2_E - steps - slope * best
 
     chunk = 128
 
     def weigh(r, acc):
         span = pl.ds(pl.multiple_of(r * chunk, chunk), chunk)
-        w = jnp.exp2(slope * (raw[span, :] - best) + shift)
+        w = jnp.exp2(slope * raw[span, :] + shift)
         weights[span, :] = w.astype(jnp.bfloat16)
         return acc + jnp.sum(w.reshape(chunk // 8, 8, samples), axis=0)
 
@@ -173,27 +171,19 @@
     store_tail(other, steps, weight_total)
 
 
-def mine_kernel(
-    turned, weights, scales, called, present, mine, own, called_part, present_part, flipped, sems
-):
+def mine_kernel(turned, weights, scales, called, present, mine, own, flipped):
     here = (lax.axis_index("panel_0") * lax.axis_size("panel_1") + lax.axis_index("panel_1")) * 2
     here = here + lax.axis_index("panel_2")
     share = own.shape[0]
     per_tile = LANES // share
     lanes = pl.ds(pl.multiple_of((here // per_tile) * LANES, LANES), LANES)
-    first = pltpu.make_async_copy(called.at[:, lanes], called_part, sems.at[0])
-    second = pltpu.make_async_copy(present.at[:, lanes], present_part, sems.at[1])
-    first.start()
-    second.start()
+    code = jnp.where(present[:, lanes] == 1, called[:, lanes].astype(jnp.float32), -1.0)
+    flipped[...] = code.T
+    own[...] = flipped[pl.ds(pl.multiple_of((here % per_tile) * share, share), share), :]
     half = turned.shape[0] // 2
     dose = jnp.dot(turned[:half, :], weights[...], preferred_element_type=jnp.float32)
     store_half(mine, dose)
     store_tail(mine, scales[0:1, :], scales[1:2, :])
-    first.wait()
-    second.wait()
-    code = jnp.where(present_part[...] == 1, called_part[...].astype(jnp.float32), -1.0)
-    flipped[...] = code.T
-    own[...] = flipped[pl.ds(pl.multiple_of((here % per_tile) * share, share), share), :]
 
 
 def pair_kernel(mine, theirs, both):
@@ -332,6 +322,7 @@
     every_count = lax.all_to_all(counts, PANEL, 0, 0, tiled=True)
 
     block = VMEM((chips, height, LANES), f32)
+    called_near, present_near = in_vmem(called), in_vmem(present)
     other, weights, scales = pl.pallas_call(
         functools.partial(impute_kernel, float(haps * devices)),
         out_shape=(block, VMEM((haps, samples), bf16), VMEM((8, samples), f32)),
@@ -339,7 +330,6 @@
         out_specs=(whole(),) * 3,
         scratch_shapes=[
             VMEM((samples, variants), bf16),
-            VMEM((samples, LANES), f32),
             VMEM((haps, samples), f32),
         ],
         cost_estimate=pl.CostEstimate(
@@ -351,28 +341,23 @@
         as_bf16,
         turned,
         every_count,
-        in_vmem(called),
-        in_vmem(present),
+        called_near,
+        present_near,
         sharpness.reshape(1, samples),
     )
     theirs = lax.ppermute(other, "panel_2", [(0, 1), (1, 0)])
     mine, own = pl.pallas_call(
         mine_kernel,
         out_shape=(block, VMEM((share, samples), f32)),
-        in_specs=[whole()] * 3 + [hbm] * 2,
+        in_specs=[whole()] * 5,
         out_specs=(whole(),) * 2,
-        scratch_shapes=[
-            VMEM((samples, LANES), jnp.int32),
-            VMEM((samples, LANES), jnp.int32),
-            VMEM((LANES, samples), f32),
-            pltpu.SemaphoreType.DMA((2,)),
-        ],
+        scratch_shapes=[VMEM((LANES, samples), f32)],
         cost_estimate=pl.CostEstimate(
             flops=samples * variants * haps, bytes_accessed=10**6, transcendentals=0
         ),
         compiler_params=pltpu.CompilerParams(vmem_limit_bytes=6 * MIB),
         name="mine",
-    )(turned, weights, scales, in_hbm(called), in_hbm(present))
+    )(turned, weights, scales, called_near, present_near)
     both = pl.pallas_call(
         pair_kernel,
         out_shape=VMEM((chips, height, LANES), f32),

time: 65.4 us -> 65 us (level)
  Pallas kernels: 12.3 us -> 11.1 us
  waiting for transfers between devices: 0.49 us -> 1.34 us
    ppermute x1, waiting for transfers between devices: 0.49 us -> 1.34 us  [on_device(): theirs = lax.ppermute(other, 'panel_2', [(0, 1), (1, 0)])]
    pallas_call x1, Pallas kernels: 2.09 us -> 1.26 us  [on_device(): pl.pallas_call(mine_kernel, out_shape=(block, VMEM((share, samples), f32)...]
  transfers between devices with their start and end apart: 1 -> 1, of which waited for: 1 -> 1; matrix products, arithmetic and copies ran while one was open for 0% -> 0% of each run, Pallas kernels for 3% -> 2%
where the time goes in v4:
time: 65 us; the launch traced here: 64.8 us
  blocking collectives  51.4 us (79%)
  Pallas kernels  11.1 us (17%)
  waiting for transfers between devices  1.34 us (2%)
  between operations  0.69 us (1%)
    all_to_all x1, blocking collectives, on_device(): parts = lax.all_to_all(both, CHIP_AXES, 0, 0, tiled=True)  21.3 us
    all_to_all x1, blocking collectives, on_device(): every_stat = lax.all_to_all(stats, 'samp', 0, 0, tiled=True)  16 us
    all_to_all x1, blocking collectives, on_device(): every_count = lax.all_to_all(counts, PANEL, 0, 0, tiled=True)  14 us
    pallas_call x1, Pallas kernels, on_device(): pl.pallas_call(functools.partial(impute_kernel, float(haps * devices)), o...  4.85 us
    pallas_call x1, Pallas kernels, on_device(): pl.pallas_call(count_kernel, out_shape=(VMEM((haps, variants), bf16), VME...  3.82 us
    ppermute x1, waiting for transfers between devices, on_device(): theirs = lax.ppermute(other, 'panel_2', [(0, 1), (1, 0)])  1.34 us
  transfers between devices with their start and end apart: 1, of which 1 were waited for; matrix products, arithmetic and copies ran while one was open for 0% of the time, Pallas kernels for 2%

profile of v4, /device:TPU:2, one launch (start us, length us, event | category | flops | bytes accessed | tf_op | source)
XLA Modules:
  0.0 64.8 jit_solution(2754284869698368393)
XLA Ops:
  0.6 0.0 copy-start.1
  0.6 0.0 copy-start
  0.7 0.0 copy-start.4
  0.7 3.8 %count.1 = (bf16[2048,1024]{1,0:T(8,128)(2,1)S(1)}, bf16[1024,2048]{1,0:T(8,128)(2,1)S(1)}, f32[32,8,128]{2,1,0:T(8,128)S(1)}) custom-call(s32[2048,1024]{1,0:T(8,128)} %panel.1), custom_call_target="tpu_custom_call" | custom-call | flops 1000000000 | bytes 8388608 | tf_op jit(solution)/shard_map/count/pallas_call | solution.py:304
  4.5 14.0 %all_to_all.15.counts = f32[32,8,128]{2,1,0:T(8,128)S(1)} all-to-all(f32[32,8,128]{2,1,0:T(8,128)S(1)} %get-tuple-element.16), channel_id=1, replica_groups=mesh['panel_0'=4,'panel_1'=4,'panel_2'=2,'samp'=8] {'panel_0','panel_1',..., dimensions={0} | all-to-all | bytes 262144 | tf_op jit(solution)/shard_map/all_to_all | solution.py:322
  18.5 0.0 copy-done.1
  18.5 0.0 copy-done
  18.5 0.0 copy-done.4
  18.5 4.9 %impute.1 = (f32[16,136,128]{2,1,0:T(8,128)S(1)}, bf16[2048,512]{1,0:T(8,128)(2,1)S(1)}, f32[8,512]{1,0:T(8,128)S(1)}) custom-call(bf16[2048,1024]{1,0:T(8,128)(2,1)S(1)} %get-tuple-element.15.as_bf16, bf16[1024,2048]{1,0:T(8,128)(2,1)S(1)} %get-tuple-element.14.turned, f32[32,8,128]{2,1,0:T(8,128)S(1)} %all_to_all.15.counts, s32[512,1024]{1,0:T(8,128)S(1)} %copy-done, ...), custom_call_target="tpu_custom_call" | custom-call | flops 3221225472 | bytes 10000000 | tf_op jit(solution)/shard_map/impute/pallas_call | solution.py:326
  23.4 0.2 collective-permute-start
  23.6 1.3 %mine.1 = (f32[16,136,128]{2,1,0:T(8,128)S(1)}, f32[32,512]{1,0:T(8,128)S(1)}) custom-call(bf16[1024,2048]{1,0:T(8,128)(2,1)S(1)} %get-tuple-element.14.turned, bf16[2048,512]{1,0:T(8,128)(2,1)S(1)} %get-tuple-element.17.weights, f32[8,512]{1,0:T(8,128)S(1)} %get-tuple-element.18.scales, s32[512,1024]{1,0:T(8,128)S(1)} %copy-done, s32[512,1024]{1,0:T(8,128)S(1)} %copy-done.1), custom_call_target="tpu_custom_call" | custom-call | flops 1073741824 | bytes 1000000 | tf_op jit(solution)/shard_map/mine/pallas_call | solution.py:349
  24.9 1.3 %collective-permute-done.theirs = f32[16,136,128]{2,1,0:T(8,128)S(1)} collective-permute-done((f32[16,136,128]{2,1,0:T(8,128)S(1)}, f32[16,136,128]{2,1,0:T(8,128)S(1)}, u32[]{:S(2)}, u32[]{:S(2)}) %collective-permute-start) | collective-permute-done | bytes 1114144 | tf_op jit(solution)/shard_map/ppermute | solution.py:348
  26.2 0.0 copy-start.2
  26.2 0.0 copy-start.3
  26.2 0.1 pair.1
  26.3 21.3 %all_to_all.16.parts = f32[16,136,128]{2,1,0:T(8,128)S(1)} all-to-all(f32[16,136,128]{2,1,0:T(8,128)S(1)} %pair.1), channel_id=1, replica_groups=mesh['panel_0'=4,'panel_1'=4,'panel_2'=2,'samp'=8] {'panel_0','panel_1'}, dimensions={0} | all-to-all | bytes 2228224 | tf_op jit(solution)/shard_map/all_to_all | solution.py:370
  47.7 0.0 copy-done.2
  47.7 0.0 copy-done.3
  47.7 0.3 dose.1
  48.0 16.0 %all_to_all.17.stats = f32[8,4,128]{2,1,0:T(4,128)S(1)} all-to-all(f32[8,4,128]{2,1,0:T(4,128)S(1)} %get-tuple-element.22), channel_id=1, replica_groups=mesh['panel_0'=4,'panel_1'=4,'panel_2'=2,'samp'=8] {'samp'}, dimensions={0} | all-to-all | bytes 32768 | tf_op jit(solution)/shard_map/all_to_all | solution.py:382
  64.0 0.7 %score.1 = (f32[1,32]{1,0:T(1,128)}, bf16[32,512]{1,0:T(8,128)(2,1)}) custom-call(f32[8,4,128]{2,1,0:T(4,128)S(1)} %all_to_all.17.stats, bf16[32,512]{1,0:T(8,128)(2,1)S(1)} %get-tuple-element.23.rounded), custom_call_target="tpu_custom_call" | custom-call | tf_op jit(solution)/shard_map/score/pallas_call | solution.py:384
Async XLA Ops:
  0.6 17.9 %copy-start.1 = (s32[512,1024]{1,0:T(8,128)S(1)}, s32[512,1024]{1,0:T(8,128)}, u32[]{:S(2)}) copy-start(s32[512,1024]{1,0:T(8,128)} %present.3) | copy-start | bytes 6291460
  0.6 17.9 %copy-start = (s32[512,1024]{1,0:T(8,128)S(1)}, s32[512,1024]{1,0:T(8,128)}, u32[]{:S(2)}) copy-start(s32[512,1024]{1,0:T(8,128)} %called.3) | copy-start | bytes 6291460
  0.7 17.9 %copy-start.4 = (f32[512]{0:T(512)S(1)}, f32[512]{0:T(512)}, u32[]{:S(2)}) copy-start(f32[512]{0:T(512)} %param.9) | copy-start | bytes 6148
  23.4 2.8 %collective-permute-start = (f32[16,136,128]{2,1,0:T(8,128)S(1)}, f32[16,136,128]{2,1,0:T(8,128)S(1)}, u32[]{:S(2)}, u32[]{:S(2)}) collective-permute-start(f32[16,136,128]{2,1,0:T(8,128)S(1)} %get-tuple-element.20), channel_id=1, source_target_pairs={{0,8},{8,0},{1,9},{9,1},{2,10},{10,2},{3,11},{11,3},{4,12},{12,4},... | collective-permute-start | bytes 3342344 | tf_op jit(solution)/shard_map/ppermute | solution.py:348
  26.2 21.5 %copy-start.2 = (f32[512]{0:T(512)S(1)}, f32[512]{0:T(512)}, u32[]{:S(2)}) copy-start(f32[512]{0:T(512)} %param.10) | copy-start | bytes 6148
  26.2 21.5 %copy-start.3 = (s32[512]{0:T(512)S(1)}, s32[512]{0:T(512)}, u32[]{:S(2)}) copy-start(s32[512]{0:T(512)} %param.11) | copy-start | bytes 6148

commit v5 on v4

--- a/solution.py
+++ b/solution.py
@@ -102,6 +102,7 @@
 
 def impute_kernel(
     haplotypes,
+    chips,
     as_bf16,
     turned,
     counts,
@@ -119,7 +120,7 @@
     freq = freq_row(counts, haplotypes, variants)
     twice = 2.0 * freq
 
-    step = 64
+    step = 128
 
     def centre(r, carry):
         span = pl.ds(pl.multiple_of(r * step, step), step)
@@ -154,7 +155,7 @@
     slope = heat * LOG2_E
     shift = peak * LOG2_E - steps - slope * best
 
-    chunk = 128
+    chunk = 256
 
     def weigh(r, acc):
         span = pl.ds(pl.multiple_of(r * chunk, chunk), chunk)
@@ -167,8 +168,16 @@
     scales[0:1, :] = steps
     scales[1:2, :] = weight_total
     dose = jnp.dot(turned[variants // 2 :, :], weights[...], preferred_element_type=jnp.float32)
-    store_half(other, dose)
-    store_tail(other, steps, weight_total)
+    share = variants // 2 // chips
+    tiles = samples // LANES
+    for t in range(tiles):
+        lanes = slice(t * LANES, (t + 1) * LANES)
+        for k in range(chips):
+            at = (k * tiles + t) * share
+            other[at : at + share, :] = dose[k * share : (k + 1) * share, lanes]
+        top = tiles * chips * share + t
+        other[top : top + 1, :] = steps[:, lanes]
+        other[top + tiles : top + tiles + 1, :] = weight_total[:, lanes]
 
 
 def mine_kernel(turned, weights, scales, called, present, mine, own, flipped):
@@ -191,17 +200,17 @@
     tiles = 4
     share = height // tiles - 2
     top = tiles * share
-    a, b = mine[0, top : top + tiles, :], theirs[0, top : top + tiles, :]
+    end = blocks * top
+    a, b = mine[0, top : top + tiles, :], theirs[end : end + tiles, :]
     steps = jnp.maximum(a, b)
     up, down = jnp.exp2(a - steps), jnp.exp2(b - steps)
-    total = up * mine[0, top + tiles :, :] + down * theirs[0, top + tiles :, :]
+    total = up * mine[0, top + tiles :, :] + down * theirs[end + tiles :, :]
     tail = jnp.concatenate([steps, total], axis=0)
     for k in range(blocks):
         for t in range(tiles):
             span = slice(t * share, (t + 1) * share)
-            both[k, span, :] = (
-                mine[k, span, :] * up[t : t + 1, :] + theirs[k, span, :] * down[t : t + 1, :]
-            )
+            x = theirs[k * top + t * share : k * top + (t + 1) * share, :]
+            both[k, span, :] = mine[k, span, :] * up[t : t + 1, :] + x * down[t : t + 1, :]
         both[k, top:, :] = tail
 
 
@@ -324,8 +333,12 @@
     block = VMEM((chips, height, LANES), f32)
     called_near, present_near = in_vmem(called), in_vmem(present)
     other, weights, scales = pl.pallas_call(
-        functools.partial(impute_kernel, float(haps * devices)),
-        out_shape=(block, VMEM((haps, samples), bf16), VMEM((8, samples), f32)),
+        functools.partial(impute_kernel, float(haps * devices), chips),
+        out_shape=(
+            VMEM((chips * tiles * share + 2 * tiles, LANES), f32),
+            VMEM((haps, samples), bf16),
+            VMEM((8, samples), f32),
+        ),
         in_specs=[whole()] * 6,
         out_specs=(whole(),) * 3,
         scratch_shapes=[

time: 65 us -> 64.8 us (level)
  no operation moved by 1% of the time
where the time goes in v5:
time: 64.8 us; the launch traced here: 64.6 us
  blocking collectives  51.4 us (79%)
  Pallas kernels  11 us (17%)
  waiting for transfers between devices  1.26 us (2%)
  between operations  0.68 us (1%)
    all_to_all x1, blocking collectives, on_device(): parts = lax.all_to_all(both, CHIP_AXES, 0, 0, tiled=True)  21.3 us
    all_to_all x1, blocking collectives, on_device(): every_stat = lax.all_to_all(stats, 'samp', 0, 0, tiled=True)  16 us
    all_to_all x1, blocking collectives, on_device(): every_count = lax.all_to_all(counts, PANEL, 0, 0, tiled=True)  14 us
    pallas_call x1, Pallas kernels, on_device(): pl.pallas_call(functools.partial(impute_kernel, float(haps * devices), ch...  4.78 us
    pallas_call x1, Pallas kernels, on_device(): pl.pallas_call(count_kernel, out_shape=(VMEM((haps, variants), bf16), VME...  3.82 us
  transfers between devices with their start and end apart: 1, of which 1 were waited for; matrix products, arithmetic and copies ran while one was open for 0% of the time, Pallas kernels for 2%

profile of v5, /device:TPU:2, one launch (start us, length us, event | category | flops | bytes accessed | tf_op | source)
XLA Modules:
  0.0 64.6 jit_solution(17083391265419223934)
XLA Ops:
  0.6 0.0 copy-start.1
  0.6 0.0 copy-start
  0.7 0.0 copy-start.4
  0.7 3.8 %count.1 = (bf16[2048,1024]{1,0:T(8,128)(2,1)S(1)}, bf16[1024,2048]{1,0:T(8,128)(2,1)S(1)}, f32[32,8,128]{2,1,0:T(8,128)S(1)}) custom-call(s32[2048,1024]{1,0:T(8,128)} %panel.1), custom_call_target="tpu_custom_call" | custom-call | flops 1000000000 | bytes 8388608 | tf_op jit(solution)/shard_map/count/pallas_call | solution.py:313
  4.5 14.0 %all_to_all.15.counts = f32[32,8,128]{2,1,0:T(8,128)S(1)} all-to-all(f32[32,8,128]{2,1,0:T(8,128)S(1)} %get-tuple-element.16), channel_id=1, replica_groups=mesh['panel_0'=4,'panel_1'=4,'panel_2'=2,'samp'=8] {'panel_0','panel_1',..., dimensions={0} | all-to-all | bytes 262144 | tf_op jit(solution)/shard_map/all_to_all | solution.py:331
  18.5 0.0 copy-done.1
  18.5 0.0 copy-done
  18.5 0.0 copy-done.4
  18.5 4.8 %impute.1 = (f32[2056,128]{1,0:T(8,128)S(1)}, bf16[2048,512]{1,0:T(8,128)(2,1)S(1)}, f32[8,512]{1,0:T(8,128)S(1)}) custom-call(bf16[2048,1024]{1,0:T(8,128)(2,1)S(1)} %get-tuple-element.15.as_bf16, bf16[1024,2048]{1,0:T(8,128)(2,1)S(1)} %get-tuple-element.14.turned, f32[32,8,128]{2,1,0:T(8,128)S(1)} %all_to_all.15.counts, s32[512,1024]{1,0:T(8,128)S(1)} %copy-done, ...), custom_call_target="tpu_custom_call" | custom-call | flops 3221225472 | bytes 10000000 | tf_op jit(solution)/shard_map/impute/pallas_call | solution.py:335
  23.3 0.2 collective-permute-start
  23.5 1.2 %mine.1 = (f32[16,136,128]{2,1,0:T(8,128)S(1)}, f32[32,512]{1,0:T(8,128)S(1)}) custom-call(bf16[1024,2048]{1,0:T(8,128)(2,1)S(1)} %get-tuple-element.14.turned, bf16[2048,512]{1,0:T(8,128)(2,1)S(1)} %get-tuple-element.17.weights, f32[8,512]{1,0:T(8,128)S(1)} %get-tuple-element.18.scales, s32[512,1024]{1,0:T(8,128)S(1)} %copy-done, s32[512,1024]{1,0:T(8,128)S(1)} %copy-done.1), custom_call_target="tpu_custom_call" | custom-call | flops 1073741824 | bytes 1000000 | tf_op jit(solution)/shard_map/mine/pallas_call | solution.py:362
  24.8 1.3 %collective-permute-done.theirs = f32[2056,128]{1,0:T(8,128)S(1)} collective-permute-done((f32[2056,128]{1,0:T(8,128)S(1)}, f32[2056,128]{1,0:T(8,128)S(1)}, u32[]{:S(2)}, u32[]{:S(2)}) %collective-permute-start) | collective-permute-done | bytes 1052704 | tf_op jit(solution)/shard_map/ppermute | solution.py:361
  26.0 0.0 copy-start.2
  26.0 0.0 copy-start.3
  26.1 0.1 pair.1
  26.2 21.3 %all_to_all.16.parts = f32[16,136,128]{2,1,0:T(8,128)S(1)} all-to-all(f32[16,136,128]{2,1,0:T(8,128)S(1)} %pair.1), channel_id=1, replica_groups=mesh['panel_0'=4,'panel_1'=4,'panel_2'=2,'samp'=8] {'panel_0','panel_1'}, dimensions={0} | all-to-all | bytes 2228224 | tf_op jit(solution)/shard_map/all_to_all | solution.py:383
  47.5 0.0 copy-done.2
  47.5 0.0 copy-done.3
  47.5 0.3 dose.1
  47.9 16.0 %all_to_all.17.stats = f32[8,4,128]{2,1,0:T(4,128)S(1)} all-to-all(f32[8,4,128]{2,1,0:T(4,128)S(1)} %get-tuple-element.22), channel_id=1, replica_groups=mesh['panel_0'=4,'panel_1'=4,'panel_2'=2,'samp'=8] {'samp'}, dimensions={0} | all-to-all | bytes 32768 | tf_op jit(solution)/shard_map/all_to_all | solution.py:395
  63.9 0.7 %score.1 = (f32[1,32]{1,0:T(1,128)}, bf16[32,512]{1,0:T(8,128)(2,1)}) custom-call(f32[8,4,128]{2,1,0:T(4,128)S(1)} %all_to_all.17.stats, bf16[32,512]{1,0:T(8,128)(2,1)S(1)} %get-tuple-element.23.rounded), custom_call_target="tpu_custom_call" | custom-call | tf_op jit(solution)/shard_map/score/pallas_call | solution.py:397
Async XLA Ops:
  0.6 17.9 %copy-start.1 = (s32[512,1024]{1,0:T(8,128)S(1)}, s32[512,1024]{1,0:T(8,128)}, u32[]{:S(2)}) copy-start(s32[512,1024]{1,0:T(8,128)} %present.3) | copy-start | bytes 6291460
  0.6 17.9 %copy-start = (s32[512,1024]{1,0:T(8,128)S(1)}, s32[512,1024]{1,0:T(8,128)}, u32[]{:S(2)}) copy-start(s32[512,1024]{1,0:T(8,128)} %called.3) | copy-start | bytes 6291460
  0.7 17.9 %copy-start.4 = (f32[512]{0:T(512)S(1)}, f32[512]{0:T(512)}, u32[]{:S(2)}) copy-start(f32[512]{0:T(512)} %param.9) | copy-start | bytes 6148
  23.3 2.8 %collective-permute-start = (f32[2056,128]{1,0:T(8,128)S(1)}, f32[2056,128]{1,0:T(8,128)S(1)}, u32[]{:S(2)}, u32[]{:S(2)}) collective-permute-start(f32[2056,128]{1,0:T(8,128)S(1)} %get-tuple-element.20), channel_id=1, source_target_pairs={{0,8},{8,0},{1,9},{9,1},{2,10},{10,2},{3,11},{11,3},{4,12},{12,4},... | collective-permute-start | bytes 3158024 | tf_op jit(solution)/shard_map/ppermute | solution.py:361
  26.0 21.5 %copy-start.2 = (f32[512]{0:T(512)S(1)}, f32[512]{0:T(512)}, u32[]{:S(2)}) copy-start(f32[512]{0:T(512)} %param.10) | copy-start | bytes 6148
  26.0 21.5 %copy-start.3 = (s32[512]{0:T(512)S(1)}, s32[512]{0:T(512)}, u32[]{:S(2)}) copy-start(s32[512]{0:T(512)} %param.11) | copy-start | bytes 6148
